TPU v7x, 256 devices: a whole 4x4x8 slice. The times are simulated.
256 devices in a mesh: batch: 4 (over y_lo, core), seq: 16 (over y_hi, z), heads: 4 (over x).
Axes of the slice: x: 4, y: 4 (y_hi: 2, y_lo: 2; y = y_hi * 2 + y_lo), z: 8, core: 2. Of those that a mesh axis runs over, the one named last changes fastest.
Arguments:
- hidden_in: bfloat16 [48, 5120], P('batch', 'seq'), may hold values from -7 to 7
- lengths: int32 [48], P('batch'), may hold values from 1 to 4096
- draft_ids: int32 [48], P('batch'), may hold values from 0 to 31999
- input_gain: float32 [5120], P('seq'), may hold values from 0.5 to 1.5
- w_query: bfloat16 [5120, 5120], P('seq', 'heads'), may hold values from -0.078125 to 0.078125
- w_latent: bfloat16 [5120, 4, 640], P('seq', 'heads'), may hold values from -0.078125 to 0.078125
- latent_cache: bfloat16 [48, 4, 4096, 640], P('batch', 'heads', 'seq'), may hold values from -1200 to 1200
- key_up: bfloat16 [4, 320, 1280], P('heads'), may hold values from -0.3125 to 0.3125
- value_up: bfloat16 [4, 320, 1280], P('heads'), may hold values from -0.3125 to 0.3125
- w_out: bfloat16 [5120, 5120], P('heads', 'seq'), may hold values from -0.078125 to 0.078125
- final_gain: float32 [5120], P('seq'), may hold values from 0.1 to 1.9
- w_vocab: bfloat16 [5120, 32000], P('seq', 'heads'), may hold values from -0.26 to 0.26
Outputs:
- new_hidden: bfloat16 [48, 5120], P('batch', 'seq')
- log_probs: float32 [48, 32000], P('batch', 'heads')
- draft_logprob: float32 [48], P('batch')
Inputs may be any that keep to these rules, and one draw needn't show every extreme that they name: `lengths`: cache positions below a request's length are its live context.
All inputs are finite; a program needn't handle non-finite values.
Results may differ from a plain program's by a relative error of at most 0.012.
The roundings to bfloat16 on the way count: a program that leaves them out, or rounds other values in their place, can miss the bound.
Values sent between devices are 32-bit elements; how exact they have to be, the bound alone decides.
A program may use at most 64 MiB of HBM per device.

v0:
```python
import math

import jax
import jax.numpy as jnp
from jax import lax
from jax.sharding import PartitionSpec as P

D = 5120
HEAD_DIM = 128
GROUP_HEADS = 10
GROUP_RANK = 320


epsilon = 1e-05
negative_fill = -1e30


def copy_for_each(value, axis):
    peers = lax.axis_size(axis)
    return lax.all_to_all(
        jnp.broadcast_to(value[None], (peers, *value.shape)), axis, 0, 0, tiled=True
    )


def of_everyone(value, axis):
    everything = copy_for_each(value, axis)
    return jnp.sum(everything, axis=0)


def together(arrays, axis):
    ends = [0]
    for a in arrays:
        ends.append(ends[-1] + a.size)
    so_far = of_everyone(jnp.concatenate([a.ravel() for a in arrays]), axis)
    return tuple((so_far[b:e].reshape(a.shape) for a, b, e in zip(arrays, ends, ends[1:])))


def all_in_one(value, axis):
    leaves = jax.tree.leaves(value)
    sequence = sorted(range(len(leaves)), key=lambda k: -leaves[k].size)
    width = (1, *leaves[sequence[0]].shape)[-1]
    lines = [
        jnp.pad(leaves[k].reshape(-1), (0, -leaves[k].size % width)).reshape(-1, width)
        for k in sequence
    ]
    both, at, found = (copy_for_each(jnp.concatenate(lines), axis), 0, {})
    for k, line in zip(sequence, lines):
        share = both[:, at : at + len(line)].reshape(len(both), -1)
        found[k] = share[:, : leaves[k].size].reshape(-1, *leaves[k].shape)
        at += len(line)
    numbers = iter(range(len(leaves)))
    return jax.tree.map(lambda _: found[next(numbers)], value)


def folded_in_pairs(pieces, combine):
    while len(jax.tree.leaves(pieces)[0]) > 1:
        pieces = jax.vmap(combine)(
            *(jax.tree.map(lambda part: part[side::2], pieces) for side in (0, 1))
        )
    return jax.tree.map(lambda part: part[0], pieces)


def merged(value, axis, combine):
    pieces = all_in_one(value, axis)
    return folded_in_pairs(pieces, combine)


def split_up(value, dim, peers):
    before, after = (value.shape[:dim], value.shape[dim + 1 :])
    return jnp.moveaxis(value.reshape(*before, peers, -1, *after), dim, 0)


def sent_and_summed(value, axis, dim):
    pieces = split_up(value, dim, lax.axis_size(axis))
    arrived = lax.all_to_all(pieces, axis, split_axis=0, concat_axis=0, tiled=True)
    return arrived.sum(axis=0)


def laid_out(pieces, dim):
    pieces = jnp.moveaxis(pieces, 0, dim)
    lengths = pieces.shape
    return pieces.reshape(*lengths[:dim], lengths[dim] * lengths[dim + 1], *lengths[dim + 2 :])


def gather_directly(value, axis, dim):
    pieces = copy_for_each(value, axis)
    return laid_out(pieces, dim)


def stats_join(left_part, right_part):
    left_max, left_total = left_part
    right_max, right_total = right_part
    joined = jnp.maximum(left_max, right_max)
    return (
        joined,
        left_total * jnp.exp(left_max - joined) + right_total * jnp.exp(right_max - joined),
    )


def vocab_join(left_part, right_part):
    left_max, left_total, left_pick = left_part
    right_max, right_total, right_pick = right_part
    joined = jnp.maximum(left_max, right_max)
    return (
        joined,
        left_total * jnp.exp(left_max - joined) + right_total * jnp.exp(right_max - joined),
        left_pick + right_pick,
    )


def vocab_stats(logits, columns, draft_ids):
    picked_local = jnp.sum(jnp.where(columns[None, :] == draft_ids[:, None], logits, 0.0), axis=1)
    local_top = jnp.max(logits, axis=1)
    return (picked_local, local_top)


def body(
    hidden_in,
    lengths,
    draft_ids,
    input_gain,
    w_query,
    w_latent,
    latent_cache,
    key_up,
    value_up,
    w_out,
    final_gain,
    w_vocab,
):
    batch_rows = hidden_in.shape[0]
    scaling = 1.0 / math.sqrt(HEAD_DIM)
    highest_prec = lax.Precision.HIGHEST
    states = hidden_in.astype(jnp.float32)
    gained = (states * input_gain).astype(jnp.bfloat16)
    query_part = jnp.dot(gained, w_query, preferred_element_type=jnp.float32)
    latent_matrix = w_latent.reshape(w_latent.shape[0], 2 * GROUP_RANK)
    latent_part = jnp.dot(gained, latent_matrix, preferred_element_type=jnp.float32)
    square_part = jnp.sum(states * states, axis=1)
    query_sum, latent_sum, square_sum = together((query_part, latent_part, square_part), "seq")
    inv_rms = lax.rsqrt(square_sum / D + epsilon)[:, None]
    query_rows = (inv_rms * query_sum).astype(jnp.bfloat16)
    latent = (inv_rms * latent_sum).astype(jnp.bfloat16)
    key_table = key_up[0].reshape(GROUP_RANK, GROUP_HEADS, HEAD_DIM)
    absorbed = jnp.einsum(
        "bhd,rhd->bhr",
        query_rows.reshape(batch_rows, GROUP_HEADS, HEAD_DIM),
        key_table,
        preferred_element_type=jnp.float32,
    ).astype(jnp.bfloat16)
    cache_rows = latent_cache[:, 0]
    local_span = cache_rows.shape[1]
    scores = (
        jnp.einsum(
            "bhr,btr->bht",
            absorbed,
            cache_rows[:, :, :GROUP_RANK],
            preferred_element_type=jnp.float32,
        )
        * scaling
    )
    positions = lax.axis_index("seq") * local_span + jnp.arange(local_span, dtype=jnp.int32)
    live_mask = positions[None, None, :] < lengths[:, None, None]
    scores = jnp.where(live_mask, scores, negative_fill)
    local_max = jnp.max(scores, axis=2)
    weights = jnp.where(live_mask, jnp.exp(scores - local_max[..., None]), 0.0)
    local_total = jnp.sum(weights, axis=2)
    local_mixed = jnp.einsum(
        "bht,btr->bhr",
        weights.astype(jnp.bfloat16),
        cache_rows[:, :, GROUP_RANK:],
        preferred_element_type=jnp.float32,
    )
    own_score = (
        jnp.einsum(
            "bhr,br->bh", absorbed, latent[:, :GROUP_RANK], preferred_element_type=jnp.float32
        )
        * scaling
    )
    own_value = latent[:, None, GROUP_RANK:].astype(jnp.float32)
    value_table = value_up[0].astype(jnp.float32).reshape(GROUP_RANK, GROUP_HEADS, HEAD_DIM)
    merged_max, merged_total = merged((local_max, local_total), "seq", stats_join)
    highest = jnp.maximum(merged_max, own_score)
    cache_scale = jnp.exp(merged_max - highest)
    own_weight = jnp.exp(own_score - highest)
    denominator = merged_total * cache_scale + own_weight
    local_scale = jnp.exp(local_max - highest)
    own_share = jnp.where(lax.axis_index("seq") == 0, own_weight, 0.0)
    latent_share = local_mixed * local_scale[..., None] + own_share[..., None] * own_value
    head_part = jnp.einsum("bhr,rhd->bhd", latent_share, value_table, precision=highest_prec)
    head_sum = of_everyone(head_part.reshape(batch_rows, GROUP_HEADS * HEAD_DIM), "seq")
    head_scaled = head_sum.reshape(batch_rows, GROUP_HEADS, HEAD_DIM) / denominator[..., None]
    head_out = head_scaled.astype(jnp.bfloat16)
    head_out = head_out.reshape(batch_rows, GROUP_HEADS * HEAD_DIM)
    attn_part = jnp.dot(head_out, w_out, preferred_element_type=jnp.float32)
    attn_sum = of_everyone(attn_part, "heads")
    updated = states + attn_sum
    new_hidden = updated.astype(jnp.bfloat16)
    final_terms = jnp.dot(
        (updated * final_gain).astype(jnp.bfloat16), w_vocab, preferred_element_type=jnp.float32
    )
    final_squares = jnp.sum(updated * updated, axis=1)
    vocab_width = w_vocab.shape[1]
    vocab_start = lax.axis_index("heads") * vocab_width
    share_sum = sent_and_summed(final_terms, "seq", 1)
    square_total = of_everyone(final_squares, "seq")
    logits = lax.rsqrt(square_total / D + epsilon)[:, None] * share_sum
    share_width = share_sum.shape[1]
    columns = (
        vocab_start + lax.axis_index("seq") * share_width + jnp.arange(share_width, dtype=jnp.int32)
    )
    picked_local, local_top = vocab_stats(logits, columns, draft_ids)
    local_sum = jnp.sum(jnp.exp(logits - local_top[:, None]), axis=1)
    top_all, total_all, picked = merged(
        (local_top, local_sum, picked_local), ("seq", "heads"), vocab_join
    )
    log_total = top_all + jnp.log(total_all)
    share_probs = logits - log_total[:, None]
    log_probs = gather_directly(share_probs, "seq", 1)
    draft_logprob = picked - log_total
    return (new_hidden, log_probs, draft_logprob)


def solution(mesh):
    return jax.shard_map(
        body,
        mesh=mesh,
        in_specs=(
            P("batch", "seq"),
            P("batch"),
            P("batch"),
            P("seq"),
            P("seq", "heads"),
            P("seq", "heads", None),
            P("batch", "heads", "seq", None),
            P("heads", None, None),
            P("heads", None, None),
            P("heads", "seq"),
            P("seq"),
            P("seq", "heads"),
        ),
        out_specs=(P("batch", "seq"), P("batch", "heads"), P("batch")),
        check_vma=False,
    )
```

profile of v0, /device:TPU:2, one launch (start us, length us, event | category | flops | bytes accessed | tf_op | source)
XLA Modules:
  0.0 202.2 jit_solution(7623787778180679578)
XLA Ops:
  0.6 0.0 copy-start
  0.7 0.9 fusion.32
  1.6 0.2 copy-done
  1.8 0.9 fusion.37
  2.7 1.2 fusion.17
  4.0 1.9 broadcast_in_dim.42
  5.9 11.2 %all-to-all-start = ((f32[16,1,23052]{2,1,0:T(1,128)}), f32[16,1,23052]{2,1,0:T(1,128)S(1)}, u32[]{:S(2)}, u32[]{:S(2)}) async-start(f32[16,1,23052]{2,1,0:T(1,128)} %broadcast_in_dim.42), calls=%async_computation | async-start | bytes 2965504 | tf_op jit(solution)/shard_map/all_to_all | solution.py:20
  17.1 1.3 copy.95
  18.4 6.3 %copy.98 = bf16[12,1,256,640]{2,3,0,1:T(8,128)(2,1)} copy(bf16[12,1,256,640]{3,2,1,0:T(8,128)(2,1)} %param.18) | data formatting | bytes 7864320 | tf_op args[6]
  24.7 1.5 copy.102
  26.2 0.1 broadcast_compare_fusion
  26.3 28.4 %all-to-all-done = f32[16,1,23052]{2,1,0:T(1,128)S(1)} async-done(((f32[16,1,23052]{2,1,0:T(1,128)}), f32[16,1,23052]{2,1,0:T(1,128)S(1)}, u32[]{:S(2)}, u32[]{:S(2)}) %all-to-all-start) | async-done | bytes 1475360 | tf_op jit(solution)/shard_map/all_to_all | solution.py:20
  54.7 0.9 reduce_sum.91
  55.7 0.1 multiply_convert_fusion
  55.8 1.5 fusion.16
  57.2 2.0 %fusion.57 = (f32[12,10]{1,0:T(8,128)S(1)}, f32[12,10,256]{2,1,0:T(8,128)S(1)}) fusion(bf16[12,256,640]{1,2,0:T(8,128)(2,1)} %bitcast.80, bf16[12,10,320]{2,0,1:T(8,128)(2,1)S(1)} %fusion.16, pred[12,256]{1,0:T(8,128)(4,1)S(1)} %broadcast_compare_fusion), kind=kOutput, calls=%fused_computation.91 | convolution fusion | flops 19752840 | bytes 2169312 | tf_op jit(solution)/shard_map/bhr,btr->bht/dot_general | solution.py:154
  59.3 0.2 fusion.20
  59.5 0.1 copy.100
  59.6 0.7 reshape.188
  60.3 4.8 %all-to-all-start.1 = ((f32[16,1,240]{2,1,0:T(1,128)}), f32[16,1,240]{2,1,0:T(1,128)S(1)}, u32[]{:S(2)}, u32[]{:S(2)}) async-start(f32[16,1,240]{2,1,0:T(1,128)} %reshape.188), calls=%async_computation.1 | async-start | bytes 32768 | tf_op jit(solution)/shard_map/all_to_all | solution.py:20
  65.2 0.1 multiply_convert_fusion.1
  65.2 0.1 slice_bitcast_fusion
  65.3 0.2 fusion.22
  65.5 9.7 %all-to-all-done.1 = f32[16,1,240]{2,1,0:T(1,128)S(1)} async-done(((f32[16,1,240]{2,1,0:T(1,128)}), f32[16,1,240]{2,1,0:T(1,128)S(1)}, u32[]{:S(2)}, u32[]{:S(2)}) %all-to-all-start.1) | async-done | bytes 15392 | tf_op jit(solution)/shard_map/all_to_all | solution.py:20
  75.1 0.5 broadcast.86
  75.6 0.7 reduce.2
  76.3 0.1 reshape.189
  76.4 0.1 fusion.56
  76.6 0.1 copy.124
  76.7 0.1 copy.125
  76.8 0.1 copy.128
  77.0 0.1 copy.129
  77.2 2.2 %fusion.7 = f32[12,10,320]{2,1,0:T(8,128)S(1)} fusion(bf16[12,256,640]{1,2,0:T(8,128)(2,1)} %bitcast.81, f32[12,320]{1,0:T(8,128)S(1)} %get-tuple-element.38, f32[12,10]{1,0:T(8,128)S(1)} %get-tuple-element.35, f32[12,10]{1,0:T(8,128)S(1)} %get-tuple-element.36, f32[12,10,256]{2,1,0:T(8,128)S(1)} %get-tuple-element.40, f32[12,10]{1,0:T(8,128)S(1)} %get-tuple-element.39, ...), kind=kOutput, calls=%fused_computation.5 | convolution fusion | flops 19868160 | bytes 2262432 | tf_op jit(solution)/shard_map/bht,btr->bhr/dot_general | solution.py:168
  79.4 1.2 convolution_bitcast_fusion
  80.6 0.0 copy-start.3
  80.7 0.0 copy-start.4
  80.7 1.2 broadcast_in_dim.49
  81.9 3.7 %all-to-all-start.2 = ((f32[16,12,1280]{2,1,0:T(8,128)}), f32[16,12,1280]{2,1,0:T(8,128)S(1)}, u32[]{:S(2)}, u32[]{:S(2)}) async-start(f32[16,12,1280]{2,1,0:T(8,128)} %broadcast_in_dim.49), calls=%async_computation.2 | async-start | bytes 2621440 | tf_op jit(solution)/shard_map/all_to_all | solution.py:20
  85.6 0.1 div.18
  85.8 32.9 %all-to-all-done.2 = f32[16,12,1280]{2,1,0:T(8,128)S(1)} async-done(((f32[16,12,1280]{2,1,0:T(8,128)}), f32[16,12,1280]{2,1,0:T(8,128)S(1)}, u32[]{:S(2)}, u32[]{:S(2)}) %all-to-all-start.2) | async-done | bytes 983072 | tf_op jit(solution)/shard_map/all_to_all | solution.py:20
  118.7 0.1 reduce_sum.93
  118.8 0.3 fusion.29
  119.1 0.1 broadcast_in_dim.50
  119.1 9.0 %all_to_all.42 = f32[4,12,320]{2,1,0:T(8,128)S(1)} all-to-all(f32[4,12,320]{2,1,0:T(8,128)S(1)} %broadcast_in_dim.50), channel_id=1, replica_groups=mesh['batch'=4,'seq'=16,'heads'=4] {'heads'}, dimensions={0} | all-to-all | bytes 122880 | tf_op jit(solution)/shard_map/all_to_all | solution.py:20
  128.1 0.7 multiply_reduce_fusion.1
  128.8 0.6 broadcast_in_dim.51
  129.4 4.3 %all-to-all-start.4 = ((f32[16,1,12]{2,1,0:T(1,128)}), f32[16,1,12]{2,1,0:T(1,128)S(1)}, u32[]{:S(2)}, u32[]{:S(2)}) async-start(f32[16,1,12]{2,1,0:T(1,128)} %broadcast_in_dim.51), calls=%async_computation.4 | async-start | bytes 16384 | tf_op jit(solution)/shard_map/all_to_all | solution.py:20
  133.7 0.0 copy-start.5
  133.8 3.3 %fusion.34 = f32[12,8000]{1,0:T(8,128)S(1)} fusion(bf16[320,8000]{1,0:T(8,128)(2,1)} %param.23, f32[320]{0:T(512)S(1)} %copy-done.4, f32[12,320]{1,0:T(8,128)S(1)} %reduce_sum.94, bf16[12,320]{1,0:T(8,128)(2,1)S(1)} %copy-done.3), kind=kOutput, calls=%fused_computation.48 | convolution fusion | flops 61455360 | bytes 5528320 | tf_op jit(solution)/shard_map/dot_general | solution.py:199
  137.0 0.4 reshape.178
  137.4 1.0 copy.163
  138.4 5.2 %all-to-all-done.4 = f32[16,1,12]{2,1,0:T(1,128)S(1)} async-done(((f32[16,1,12]{2,1,0:T(1,128)}), f32[16,1,12]{2,1,0:T(1,128)S(1)}, u32[]{:S(2)}, u32[]{:S(2)}) %all-to-all-start.4) | async-done | bytes 800 | tf_op jit(solution)/shard_map/all_to_all | solution.py:20
  143.6 4.4 %all-to-all-start.5 = ((f32[16,12,500]{2,1,0:T(8,128)}), f32[16,12,500]{2,1,0:T(8,128)S(1)}, u32[]{:S(2)}, u32[]{:S(2)}) async-start(f32[16,12,500]{2,1,0:T(8,128)} %bitcast.79), calls=%async_computation.5 | async-start | bytes 1048576 | tf_op jit(solution)/shard_map/all_to_all | solution.py:75
  148.1 14.9 %all-to-all-done.5 = f32[16,12,500]{2,1,0:T(8,128)S(1)} async-done(((f32[16,12,500]{2,1,0:T(8,128)}), f32[16,12,500]{2,1,0:T(8,128)S(1)}, u32[]{:S(2)}, u32[]{:S(2)}) %all-to-all-start.5) | async-done | bytes 384032 | tf_op jit(solution)/shard_map/all_to_all | solution.py:75
  163.0 0.2 multiply_reduce_fusion
  163.2 0.2 exponential_reduce_fusion
  163.5 18.7 %all_to_all.43 = f32[64,3,12]{2,1,0:T(4,128)S(1)} all-to-all(f32[64,3,12]{2,1,0:T(4,128)S(1)} %broadcast_in_dim.53), channel_id=1, replica_groups=mesh['batch'=4,'seq'=16,'heads'=4] {'seq','heads'}, dimensions={0} | all-to-all | bytes 18432 | tf_op jit(solution)/shard_map/all_to_all | solution.py:20
  182.2 0.1 fusion.53
  182.9 0.5 bitcast_subtract_fusion.1
  183.5 0.1 multiply_subtract_fusion
  183.6 0.1 broadcast_in_dim.96
  183.6 17.3 %all_to_all.44 = f32[16,12,500]{2,1,0:T(8,128)S(1)} all-to-all(f32[16,12,500]{2,1,0:T(8,128)S(1)} %broadcast_in_dim.96), channel_id=1, replica_groups=mesh['batch'=4,'seq'=16,'heads'=4] {'seq'}, dimensions={0} | all-to-all | bytes 768000 | tf_op jit(solution)/shard_map/all_to_all | solution.py:20
  200.9 0.2 copy.112
  201.1 1.1 reshape.184
  (77 shorter events, 1.1 us)
Async XLA Ops:
  0.6 1.2 copy-start
  0.6 16.4 %copy-start.1 = (bf16[1,320,1280]{2,1,0:T(8,128)(2,1)S(1)}, bf16[1,320,1280]{2,1,0:T(8,128)(2,1)}, u32[]{:S(2)}) copy-start(bf16[1,320,1280]{2,1,0:T(8,128)(2,1)} %param.19) | copy-start | bytes 2457604
  5.9 48.8 %all-to-all-start = ((f32[16,1,23052]{2,1,0:T(1,128)}), f32[16,1,23052]{2,1,0:T(1,128)S(1)}, u32[]{:S(2)}, u32[]{:S(2)}) async-start(f32[16,1,23052]{2,1,0:T(1,128)} %broadcast_in_dim.42), calls=%async_computation | async-start | bytes 2965504 | tf_op jit(solution)/shard_map/all_to_all | solution.py:20
  18.4 7.9 %copy-start.6 = (s32[12]{0:T(128)S(1)}, s32[12]{0:T(128)}, u32[]{:S(2)}) copy-start(s32[12]{0:T(128)} %param.13) | copy-start | bytes 148
  60.3 14.8 %all-to-all-start.1 = ((f32[16,1,240]{2,1,0:T(1,128)}), f32[16,1,240]{2,1,0:T(1,128)S(1)}, u32[]{:S(2)}, u32[]{:S(2)}) async-start(f32[16,1,240]{2,1,0:T(1,128)} %reshape.188), calls=%async_computation.1 | async-start | bytes 32768 | tf_op jit(solution)/shard_map/all_to_all | solution.py:20
  79.4 39.3 %copy-start.2 = (bf16[1280,320]{0,1:T(8,128)(2,1)S(1)}, bf16[1280,320]{0,1:T(8,128)(2,1)}, u32[]{:S(2)}) copy-start(bf16[1280,320]{0,1:T(8,128)(2,1)} %param.21) | copy-start | bytes 2457604
  80.6 47.5 %copy-start.3 = (bf16[12,320]{1,0:T(8,128)(2,1)S(1)}, bf16[12,320]{1,0:T(8,128)(2,1)}, u32[]{:S(2)}) copy-start(bf16[12,320]{1,0:T(8,128)(2,1)} %param.12) | copy-start | bytes 23044
  80.7 53.1 %copy-start.4 = (f32[320]{0:T(512)S(1)}, f32[320]{0:T(512)}, u32[]{:S(2)}) copy-start(f32[320]{0:T(512)} %param.22) | copy-start | bytes 3844
  81.9 36.8 %all-to-all-start.2 = ((f32[16,12,1280]{2,1,0:T(8,128)}), f32[16,12,1280]{2,1,0:T(8,128)S(1)}, u32[]{:S(2)}, u32[]{:S(2)}) async-start(f32[16,12,1280]{2,1,0:T(8,128)} %broadcast_in_dim.49), calls=%async_computation.2 | async-start | bytes 2621440 | tf_op jit(solution)/shard_map/all_to_all | solution.py:20
  129.4 14.2 %all-to-all-start.4 = ((f32[16,1,12]{2,1,0:T(1,128)}), f32[16,1,12]{2,1,0:T(1,128)S(1)}, u32[]{:S(2)}, u32[]{:S(2)}) async-start(f32[16,1,12]{2,1,0:T(1,128)} %broadcast_in_dim.51), calls=%async_computation.4 | async-start | bytes 16384 | tf_op jit(solution)/shard_map/all_to_all | solution.py:20
  133.7 29.5 %copy-start.5 = (s32[12]{0:T(128)S(1)}, s32[12]{0:T(128)}, u32[]{:S(2)}) copy-start(s32[12]{0:T(128)} %param.14) | copy-start | bytes 148
  143.6 19.3 %all-to-all-start.5 = ((f32[16,12,500]{2,1,0:T(8,128)}), f32[16,12,500]{2,1,0:T(8,128)S(1)}, u32[]{:S(2)}, u32[]{:S(2)}) async-start(f32[16,12,500]{2,1,0:T(8,128)} %bitcast.79), calls=%async_computation.5 | async-start | bytes 1048576 | tf_op jit(solution)/shard_map/all_to_all | solution.py:75
where the time goes:
time: 203 us; the launch traced here: 202 us
  waiting for transfers between devices  91.1 us (45%)
  blocking collectives  45 us (22%)
  starting transfers between devices  28.4 us (14%)
  local copies, waits for them, and re-layouts  18.8 us (9%)
  matrix products  12.7 us (6%)
  other arithmetic  5.18 us (3%)
    all_to_all x4, waiting for transfers between devices, copy_for_each(): lax.all_to_all(jnp.broadcast_to(value[None], (peers, *value.shape)), axis...  76.2 us
    all_to_all x3, blocking collectives, copy_for_each(): lax.all_to_all(jnp.broadcast_to(value[None], (peers, *value.shape)), axis...  45 us
    all_to_all x4, starting transfers between devices, copy_for_each(): lax.all_to_all(jnp.broadcast_to(value[None], (peers, *value.shape)), axis...  24 us
    all_to_all x1, waiting for transfers between devices, sent_and_summed(): lax.all_to_all(pieces, axis, split_axis=0, concat_axis=0, tiled=True)  14.9 us
    unnamed x28, local copies, waits for them, and re-layouts  10.8 us
    all_to_all x1, starting transfers between devices, sent_and_summed(): lax.all_to_all(pieces, axis, split_axis=0, concat_axis=0, tiled=True)  4.39 us
  transfers between devices with their start and end apart: 5, of which 5 were waited for; matrix products, arithmetic and copies ran while one was open for 7% of the time, Pallas kernels for 0%

commit v1 on v0

v1 whole, which is shorter than its diff:
```python
import functools
import math

import jax
import jax.numpy as jnp
from jax import lax
from jax.experimental import pallas as pl
from jax.experimental.pallas import tpu as pltpu
from jax.sharding import PartitionSpec as P

D = 5120
HEAD_DIM = 128
GROUP_HEADS = 10
RANK = 320
SEQ = 16
ROWS = 12
SPAN = 256
WIDE = 512
VOCAB_LOCAL = 8000
PIECES = 15
TAIL = VOCAB_LOCAL - 15 * WIDE

MESH = pl.DeviceIdType.MESH
f32 = jnp.float32
bf16 = jnp.bfloat16
epsilon = 1e-05
negative_fill = -1e30
scaling = 1.0 / math.sqrt(HEAD_DIM)

QUERY_SUM, QUERY_ALL, HEAD_SUM, HEAD_ALL, SQUARES, VOCAB_SUM, VOCAB_ALL = range(7)


def owner_of_head(k):
    return lax.div(k * 8, 5)


def head_of_owner(s):
    return lax.div(s * 5 + 7, 8)


def owns_head(s):
    return owner_of_head(head_of_owner(s)) == s


def iota(shape, dim):
    return lax.broadcasted_iota(jnp.int32, shape, dim)


def as_row(column):
    spread = jnp.where(iota((16, 128), 0) == iota((16, 128), 1), column, 0.0)
    return jnp.sum(spread, axis=0, keepdims=True)


def as_column(row, picks):
    return jnp.sum(jnp.where(picks == iota(picks.shape, 1), row, 0.0), axis=1, keepdims=True)


def kernel(
    heads_size,
    hidden, lengths, drafts, gain, wq, wl, cache, ku, vu, wo, fgain, wv,
    new_hidden, log_probs, draft_out,
    hid_v, len_s, draft_s, gain_v, wq_v, wl_v, cache_v, ku_v, vu_v, wo_v, fgain_v, wv_v,
    states_v,
    qa_send, qa_recv, qa_all,
    absorbed_v, mixed_v,
    hb_send, hb_recv, hb_all, own_v,
    at_send, at_recv,
    sq_send, sq_recv,
    vd_send, vd_recv, vd_all,
    st_send, st_recv,
    load_sem, send_sem, recv_sem, x_send_sem, x_recv_sem,
):
    me = lax.axis_index("seq")
    hme = lax.axis_index("heads")

    loads = [
        (hidden, hid_v), (gain, gain_v), (lengths, len_s), (drafts, draft_s), (fgain, fgain_v),
        (wq, wq_v), (wl, wl_v), (ku, ku_v), (cache, cache_v), (vu, vu_v.at[pl.ds(64, RANK)]),
        (wo, wo_v), (wv, wv_v),
    ]
    loads = [pltpu.make_async_copy(a, b, load_sem.at[i]) for i, (a, b) in enumerate(loads)]
    l_hid, l_gain, l_len, l_draft, l_fgain, l_wq, l_wl, l_ku, l_cache, l_vu, l_wo, l_wv = loads
    for load in loads:
        load.start()

    barrier = pltpu.get_barrier_semaphore()

    @pl.loop(1, SEQ)
    def _(j):
        pl.semaphore_signal(
            barrier, inc=1, device_id={"seq": lax.rem(me + j, SEQ)}, device_id_type=MESH
        )

    for j in range(1, heads_size):
        pl.semaphore_signal(
            barrier, inc=1, device_id={"heads": lax.rem(hme + j, heads_size)}, device_id_type=MESH
        )

    def over_seq(phase, src, dst, peer):
        return pltpu.make_async_remote_copy(
            src_ref=src, dst_ref=dst,
            send_sem=send_sem.at[phase, peer], recv_sem=recv_sem.at[phase, me],
            device_id={"seq": peer}, device_id_type=MESH,
        )

    def arrived(phase, ref, peer):
        pltpu.make_async_copy(ref, ref, recv_sem.at[phase, peer]).wait()

    def sent(phase, ref, peer):
        pltpu.make_async_copy(ref, ref, send_sem.at[phase, peer]).wait()

    def rows16(ref, i):
        return ref.at[pl.ds(pl.multiple_of(i * 16, 16), 16)]

    vu_v[0:64, :] = jnp.zeros((64, GROUP_HEADS * HEAD_DIM), bf16)
    absorbed_v[...] = jnp.zeros_like(absorbed_v)
    mixed_v[...] = jnp.zeros_like(mixed_v)
    states_v[...] = jnp.zeros_like(states_v)
    l_hid.wait()
    l_gain.wait()
    states_v[0:ROWS, :] = hid_v[...].astype(f32)
    states = states_v[...]
    gained = (states * gain_v[...]).astype(bf16)
    squares = as_row(jnp.sum(states * states, axis=1, keepdims=True))
    row = iota((16, 128), 0)
    l_wq.wait()
    query_part = jnp.dot(gained, wq_v[...], preferred_element_type=f32)
    for k in range(10):
        part = query_part[:, k * 128 : (k + 1) * 128]
        qa_send[k * 16 : (k + 1) * 16, :] = jnp.where(row == 12, squares, part)
    l_wl.wait()
    latent_part = jnp.dot(gained, wl_v[...], preferred_element_type=f32)
    for k in range(5):
        part = latent_part[:, k * 128 : (k + 1) * 128]
        qa_send[(k + 10) * 16 : (k + 11) * 16, :] = jnp.where(row == 12, squares, part)

    pl.semaphore_wait(barrier, SEQ - 1 + heads_size - 1)

    @pl.loop(1, SEQ)
    def _(j):
        peer = lax.rem(me + j, SEQ)

        @pl.when(peer < PIECES)
        def _():
            over_seq(QUERY_SUM, rows16(qa_send, peer), rows16(qa_recv, me), peer).start()

    @pl.when(me < PIECES)
    def _():
        qa_recv[pl.ds(pl.multiple_of(me * 16, 16), 16), :] = qa_send[
            pl.ds(pl.multiple_of(me * 16, 16), 16), :
        ]

        @pl.loop(1, SEQ)
        def _(j):
            peer = lax.rem(me + j, SEQ)
            arrived(QUERY_SUM, rows16(qa_recv, peer), peer)

        total = qa_recv[0:16, :]
        for i in range(1, SEQ):
            total = total + qa_recv[i * 16 : (i + 1) * 16, :]
        mean = as_column(total[12:13, :], row) / D
        done = (lax.rsqrt(mean + epsilon) * total).astype(bf16).astype(f32)
        qa_all[pl.ds(pl.multiple_of(me * 16, 16), 16), :] = jnp.where(row < ROWS, done, 0.0)

        @pl.loop(1, SEQ)
        def _(j):
            peer = lax.rem(me + j, SEQ)
            over_seq(QUERY_ALL, rows16(qa_all, me), rows16(qa_all, me), peer).start()

    @pl.loop(1, SEQ)
    def _(j):
        peer = lax.rem(me + j, SEQ)

        @pl.when(peer < PIECES)
        def _():
            arrived(QUERY_ALL, rows16(qa_all, peer), peer)

    l_ku.wait()
    for k in range(GROUP_HEADS):
        query = qa_all[k * 16 : (k + 1) * 16, :].astype(bf16)
        absorbed = lax.dot_general(
            query, ku_v[:, k * 128 : (k + 1) * 128], (((1,), (1,)), ((), ())),
            preferred_element_type=f32,
        )
        absorbed = absorbed.astype(bf16).astype(f32)
        absorbed_v[0, k * 16 : (k + 1) * 16, :] = absorbed[:, 0:128]
        absorbed_v[1, k * 16 : (k + 1) * 16, :] = absorbed[:, 128:256]
        absorbed_v[2, k * 16 : (k + 1) * 16, 0:64] = absorbed[:, 256:320]

    l_len.wait()
    l_cache.wait()
    positions = me * SPAN + iota((16, SPAN), 1)
    lane = iota((16, 128), 1)
    maxima = jnp.zeros((16, 128), f32)
    totals = jnp.zeros((16, 128), f32)
    scores = []
    for b in range(ROWS):
        one = jnp.concatenate(
            [absorbed_v[t, pl.ds(b, 16, stride=16), :] for t in range(3)], axis=1
        ).astype(bf16)
        scores.append(
            lax.dot_general(
                one, cache_v[b, :, 0:384], (((1,), (1,)), ((), ())), preferred_element_type=f32
            )
        )
    weights = []
    for b in range(ROWS):
        live = positions < len_s[b]
        score = jnp.where(live, scores[b] * scaling, negative_fill)
        top = jnp.max(score, axis=1, keepdims=True)
        weight = jnp.where(live, jnp.exp(score - top), 0.0)
        maxima = jnp.where(lane == b, top, maxima)
        totals = jnp.where(lane == b, jnp.sum(weight, axis=1, keepdims=True), totals)
        weights.append(weight.astype(bf16))
    for b in range(ROWS):
        mixed = jnp.dot(weights[b], cache_v[b, :, 256:640], preferred_element_type=f32)
        for t in range(3):
            mixed_v[t, b * 16 : (b + 1) * 16, :] = mixed[:, t * 128 : (t + 1) * 128]

    l_vu.wait()
    for k in range(GROUP_HEADS):
        mixed = jnp.concatenate(
            [mixed_v[t, pl.ds(k, 16, stride=16), :] for t in range(3)], axis=1
        )
        high = mixed.astype(bf16)
        low = (mixed - high.astype(f32)).astype(bf16)
        both = jnp.dot(
            jnp.concatenate([high, low], axis=0), vu_v[:, k * 128 : (k + 1) * 128],
            preferred_element_type=f32,
        )
        part = both[0:16] + both[16:32]
        part = jnp.where(row == 12, maxima[k : k + 1, :], part)
        part = jnp.where(row == 13, totals[k : k + 1, :], part)
        hb_send[k * 16 : (k + 1) * 16, :] = part

    @pl.loop(1, SEQ)
    def _(j):
        peer = lax.rem(me + j, SEQ)

        @pl.when(owns_head(peer))
        def _():
            over_seq(
                HEAD_SUM, rows16(hb_send, head_of_owner(peer)), rows16(hb_recv, me), peer
            ).start()

    own_key = jnp.concatenate([qa_all[(10 + t) * 16 : (11 + t) * 16, :] for t in range(3)], axis=1)
    own_value = jnp.concatenate(
        [qa_all[(12 + t) * 16 : (13 + t) * 16, :] for t in range(3)], axis=1
    ).astype(bf16)
    own = jnp.dot(own_value, vu_v[...], preferred_element_type=f32)
    for k in range(GROUP_HEADS):
        own_v[k * 16 : (k + 1) * 16, :] = own[:, k * 128 : (k + 1) * 128]

    @pl.when(owns_head(me))
    def _():
        k = head_of_owner(me)
        mine = pl.ds(pl.multiple_of(k * 16, 16), 16)
        hb_recv[pl.ds(pl.multiple_of(me * 16, 16), 16), :] = hb_send[mine, :]
        absorbed = jnp.concatenate([absorbed_v[t, mine, :] for t in range(3)], axis=1)
        own_score = jnp.sum(absorbed * own_key, axis=1, keepdims=True) * scaling

        @pl.loop(1, SEQ)
        def _(j):
            peer = lax.rem(me + j, SEQ)
            arrived(HEAD_SUM, rows16(hb_recv, peer), peer)

        tops = hb_recv[pl.ds(12, 16, stride=16), :].T[0:16, :]
        sums = hb_recv[pl.ds(13, 16, stride=16), :].T[0:16, :]
        highest = jnp.maximum(jnp.max(tops, axis=1, keepdims=True), own_score)
        shares = jnp.exp(tops - highest)
        own_weight = jnp.exp(own_score - highest)
        denominator = jnp.sum(shares * sums, axis=1, keepdims=True) + own_weight
        total = own_weight * own_v[mine, :]
        for i in range(SEQ):
            total = total + shares[:, i : i + 1] * hb_recv[i * 16 : (i + 1) * 16, :]
        head_out = (total / denominator).astype(bf16).astype(f32)
        hb_all[mine, :] = jnp.where(row < ROWS, head_out, 0.0)

        @pl.loop(1, SEQ)
        def _(j):
            peer = lax.rem(me + j, SEQ)
            over_seq(HEAD_ALL, rows16(hb_all, k), rows16(hb_all, k), peer).start()

    @pl.loop(1, SEQ)
    def _(j):
        peer = lax.rem(me + j, SEQ)

        @pl.when(owns_head(peer))
        def _():
            arrived(HEAD_ALL, rows16(hb_all, head_of_owner(peer)), peer)

    def over_heads(phase, src, dst, peer):
        return pltpu.make_async_remote_copy(
            src_ref=src, dst_ref=dst,
            send_sem=x_send_sem.at[phase, peer], recv_sem=x_recv_sem.at[phase, hme],
            device_id={"heads": peer}, device_id_type=MESH,
        )

    l_wo.wait()
    heads_out = jnp.concatenate(
        [hb_all[k * 16 : (k + 1) * 16, :] for k in range(GROUP_HEADS)], axis=1
    ).astype(bf16)
    at_send[...] = jnp.dot(heads_out, wo_v[...], preferred_element_type=f32)
    for j in range(1, heads_size):
        peer = lax.rem(hme + j, heads_size)
        over_heads(0, at_send, at_recv.at[hme], peer).start()
    at_recv[hme] = at_send[...]
    l_fgain.wait()
    for j in range(1, heads_size):
        peer = lax.rem(hme + j, heads_size)
        pltpu.make_async_copy(at_send, at_send, x_recv_sem.at[0, peer]).wait()
    attn = at_recv[0]
    for h in range(1, heads_size):
        attn = attn + at_recv[h]
    updated = states_v[...] + attn
    new_hidden[...] = updated[0:ROWS].astype(bf16)
    sq_send[...] = as_row(jnp.sum(updated * updated, axis=1, keepdims=True))

    @pl.loop(1, SEQ)
    def _(j):
        peer = lax.rem(me + j, SEQ)
        over_seq(SQUARES, sq_send, sq_recv.at[me], peer).start()

    scaled = updated * fgain_v[...]
    bottom = scaled[8:16]
    bottom = jnp.where(iota(bottom.shape, 0) < 4, bottom, pltpu.roll(bottom, 4, 0))
    twice = jnp.concatenate([scaled[0:8], bottom], axis=0).astype(bf16)
    l_wv.wait()
    lower = iota((8, 256), 0) < 4

    def piece(c):
        terms = jnp.dot(
            twice, wv_v[:, pl.ds(pl.multiple_of(c * WIDE, WIDE), WIDE)], preferred_element_type=f32
        )
        vd_send[c, :, 0:512] = terms[0:8]
        vd_send[c, :, 512:768] = jnp.where(lower, terms[8:16, 0:256], terms[8:16, 256:512])

    def last_piece():
        terms = jnp.dot(twice, wv_v[:, 15 * WIDE : VOCAB_LOCAL], preferred_element_type=f32)
        vd_send[15] = jnp.zeros((8, 768), f32)
        vd_send[15, :, 0:TAIL] = terms[0:8]
        vd_send[15, 0:4, 512:768] = terms[8:12, 0:256]
        vd_send[15, 4:8, 512 : 512 + TAIL - 256] = terms[12:16, 256:TAIL]

    def any_piece(c):
        @pl.when(c < 15)
        def _():
            piece(c)

        @pl.when(c == 15)
        def _():
            last_piece()

    @pl.loop(1, SEQ)
    def _(j):
        peer = lax.rem(me + j, SEQ)
        any_piece(peer)
        over_seq(VOCAB_SUM, vd_send.at[peer], vd_recv.at[me], peer).start()

    any_piece(me)
    vd_recv[me] = vd_send[me]
    sq_recv[me] = sq_send[...]

    @pl.loop(1, SEQ)
    def _(j):
        peer = lax.rem(me + j, SEQ)
        arrived(SQUARES, sq_recv.at[peer], peer)
        arrived(VOCAB_SUM, vd_recv.at[peer], peer)

    square_total = sq_recv[0]
    share = vd_recv[0]
    for i in range(1, SEQ):
        square_total = square_total + sq_recv[i]
        share = share + vd_recv[i]
    inv = lax.rsqrt(square_total / D + epsilon)
    sub = iota((8, 128), 0)
    inv_top = as_column(inv, sub)
    inv_bottom = as_column(inv, 8 + lax.rem(sub, 4))
    spot = iota((8, 512), 1)
    spot_bottom = iota((8, 256), 1) + jnp.where(lower, 0, 256)
    limit = VOCAB_LOCAL - me * WIDE
    vd_all[me, :, 0:512] = jnp.where(spot < limit, share[:, 0:512] * inv_top, negative_fill)
    vd_all[me, :, 512:768] = jnp.where(
        spot_bottom < limit, share[:, 512:768] * inv_bottom, negative_fill
    )

    @pl.loop(1, SEQ)
    def _(j):
        peer = lax.rem(me + j, SEQ)
        over_seq(VOCAB_ALL, vd_all.at[me], vd_all.at[me], peer).start()

    l_draft.wait()
    sub1 = iota((8, 1), 0)
    draft_top = jnp.zeros((8, 1), jnp.int32)
    draft_bottom = jnp.zeros((8, 1), jnp.int32)
    for b in range(8):
        draft_top = jnp.where(sub1 == b, draft_s[b], draft_top)
    for b in range(4):
        draft_bottom = jnp.where(lax.rem(sub1, 4) == b, draft_s[8 + b], draft_bottom)
    draft_top = draft_top - hme * VOCAB_LOCAL
    draft_bottom = draft_bottom - hme * VOCAB_LOCAL

    @pl.loop(1, SEQ)
    def _(j):
        peer = lax.rem(me + j, SEQ)
        arrived(VOCAB_ALL, vd_all.at[peer], peer)

    top = vd_all[0]
    for c in range(1, SEQ):
        top = jnp.maximum(top, vd_all[c])
    max_top = jnp.max(top[:, 0:512], axis=1, keepdims=True)
    max_bottom = jnp.max(top[:, 512:768], axis=1, keepdims=True)
    max_bottom = jnp.maximum(max_bottom, pltpu.roll(jnp.broadcast_to(max_bottom, (8, 128)), 4, 0)[:, 0:1])
    sum_top = jnp.zeros((8, 512), f32)
    sum_bottom = jnp.zeros((8, 256), f32)
    pick_top = jnp.zeros((8, 512), f32)
    pick_bottom = jnp.zeros((8, 256), f32)
    for c in range(SEQ):
        high = vd_all[c, :, 0:512]
        low = vd_all[c, :, 512:768]
        sum_top = sum_top + jnp.exp(high - max_top)
        sum_bottom = sum_bottom + jnp.exp(low - max_bottom)
        inside = c * WIDE + spot
        pick_top = pick_top + jnp.where((inside == draft_top) & (inside < VOCAB_LOCAL), high, 0.0)
        inside = c * WIDE + spot_bottom
        pick_bottom = pick_bottom + jnp.where(
            (inside == draft_bottom) & (inside < VOCAB_LOCAL), low, 0.0
        )

    def folded(value):
        column = jnp.sum(value, axis=1, keepdims=True)
        wide = jnp.broadcast_to(column, (8, 128))
        return (wide + pltpu.roll(wide, 4, 0))[:, 0:1]

    lane8 = iota((8, 128), 1)
    block = jnp.zeros((8, 128), f32)
    for i, column in enumerate((
        max_top, max_bottom,
        jnp.sum(sum_top, axis=1, keepdims=True), folded(sum_bottom),
        jnp.sum(pick_top, axis=1, keepdims=True), folded(pick_bottom),
    )):
        block = jnp.where(lane8 == i, column, block)
    st_send[...] = block
    for j in range(1, heads_size):
        peer = lax.rem(hme + j, heads_size)
        over_heads(1, st_send, st_recv.at[hme], peer).start()
    st_recv[hme] = block
    for j in range(1, heads_size):
        peer = lax.rem(hme + j, heads_size)
        pltpu.make_async_copy(st_send, st_send, x_recv_sem.at[1, peer]).wait()
    blocks = [st_recv[h] for h in range(heads_size)]

    def closing(at):
        tops = [x[:, at : at + 1] for x in blocks]
        highest = functools.reduce(jnp.maximum, tops)
        total = sum(x[:, 2 + at : 3 + at] * jnp.exp(t - highest) for x, t in zip(blocks, tops))
        picked = sum(x[:, 4 + at : 5 + at] for x in blocks)
        log_total = highest + jnp.log(total)
        return log_total, picked - log_total

    log_top, picked_top = closing(0)
    log_bottom, picked_bottom = closing(1)
    pick = jnp.where(lane8 == sub, picked_top, 0.0) + jnp.where(
        (lane8 == sub + 8) & (sub < 4), picked_bottom, 0.0
    )
    draft_out[...] = jnp.sum(pick, axis=0, keepdims=True)
    for c in range(SEQ):
        at = c * WIDE
        width = min(WIDE, VOCAB_LOCAL - at)
        log_probs[0:8, at : at + width] = vd_all[c, :, 0:width] - log_top
        low = vd_all[c, :, 512:768] - log_bottom
        log_probs[8:12, at : at + 256] = low[0:4]
        rest = min(256, width - 256)
        log_probs[8:12, at + 256 : at + 256 + rest] = pltpu.roll(low, 4, 0)[0:4, 0:rest]

    @pl.loop(1, SEQ)
    def _(j):
        peer = lax.rem(me + j, SEQ)

        @pl.when(peer < PIECES)
        def _():
            sent(QUERY_SUM, rows16(qa_send, peer), peer)

        @pl.when(me < PIECES)
        def _():
            sent(QUERY_ALL, rows16(qa_all, me), peer)

        @pl.when(owns_head(peer))
        def _():
            sent(HEAD_SUM, rows16(hb_send, head_of_owner(peer)), peer)

        @pl.when(owns_head(me))
        def _():
            sent(HEAD_ALL, rows16(hb_all, head_of_owner(me)), peer)

        sent(SQUARES, sq_send, peer)
        sent(VOCAB_SUM, vd_send.at[peer], peer)
        sent(VOCAB_ALL, vd_all.at[me], peer)

    for j in range(1, heads_size):
        peer = lax.rem(hme + j, heads_size)
        pltpu.make_async_copy(at_send, at_send, x_send_sem.at[0, peer]).wait()
        pltpu.make_async_copy(st_send, st_send, x_send_sem.at[1, peer]).wait()


def solution(mesh):
    heads_size = mesh.shape["heads"]

    def body(hidden, lengths, drafts, gain, wq, wl, cache, ku, vu, wo, fgain, wv):
        any_spec = pl.BlockSpec(memory_space=pl.ANY)
        vmem = pl.BlockSpec(memory_space=pltpu.VMEM)
        width = GROUP_HEADS * HEAD_DIM
        new_hidden, log_probs, draft = pl.pallas_call(
            functools.partial(kernel, heads_size),
            name="decode_step",
            out_shape=(
                jax.ShapeDtypeStruct((ROWS, RANK), bf16),
                jax.ShapeDtypeStruct((ROWS, VOCAB_LOCAL), f32),
                jax.ShapeDtypeStruct((1, 128), f32),
            ),
            in_specs=[any_spec] * 12,
            out_specs=(vmem, vmem, vmem),
            scratch_shapes=[
                pltpu.VMEM((ROWS, RANK), bf16),
                pltpu.SMEM((ROWS,), jnp.int32),
                pltpu.SMEM((ROWS,), jnp.int32),
                pltpu.VMEM((1, RANK), f32),
                pltpu.VMEM((RANK, width), bf16),
                pltpu.VMEM((RANK, 2 * RANK), bf16),
                pltpu.VMEM((ROWS, SPAN, 2 * RANK), bf16),
                pltpu.VMEM((RANK, width), bf16),
                pltpu.VMEM((384, width), bf16),
                pltpu.VMEM((width, RANK), bf16),
                pltpu.VMEM((1, RANK), f32),
                pltpu.VMEM((RANK, VOCAB_LOCAL), bf16),
                pltpu.VMEM((16, RANK), f32),
                pltpu.VMEM((256, 128), f32),
                pltpu.VMEM((256, 128), f32),
                pltpu.VMEM((256, 128), f32),
                pltpu.VMEM((3, 256, 128), f32),
                pltpu.VMEM((3, 256, 128), f32),
                pltpu.VMEM((160, 128), f32),
                pltpu.VMEM((256, 128), f32),
                pltpu.VMEM((160, 128), f32),
                pltpu.VMEM((160, 128), f32),
                pltpu.VMEM((16, RANK), f32),
                pltpu.VMEM((heads_size, 16, RANK), f32),
                pltpu.VMEM((1, 128), f32),
                pltpu.VMEM((SEQ, 1, 128), f32),
                pltpu.VMEM((SEQ, 8, 768), f32),
                pltpu.VMEM((SEQ, 8, 768), f32),
                pltpu.VMEM((SEQ, 8, 768), f32),
                pltpu.VMEM((8, 128), f32),
                pltpu.VMEM((heads_size, 8, 128), f32),
                pltpu.SemaphoreType.DMA((12,)),
                pltpu.SemaphoreType.DMA((7, SEQ)),
                pltpu.SemaphoreType.DMA((7, SEQ)),
                pltpu.SemaphoreType.DMA((2, heads_size)),
                pltpu.SemaphoreType.DMA((2, heads_size)),
            ],
            compiler_params=pltpu.CompilerParams(
                collective_id=0, has_side_effects=True, vmem_limit_bytes=48 * 1024 * 1024
            ),
        )(
            hidden, lengths, drafts, gain.reshape(1, RANK), wq, wl.reshape(RANK, 2 * RANK),
            cache.reshape(ROWS, SPAN, 2 * RANK), ku.reshape(RANK, width), vu.reshape(RANK, width),
            wo, fgain.reshape(1, RANK), wv,
        )
        return new_hidden, log_probs, draft[0, :ROWS]

    return jax.shard_map(
        body,
        mesh=mesh,
        in_specs=(
            P("batch", "seq"), P("batch"), P("batch"), P("seq"), P("seq", "heads"),
            P("seq", "heads", None), P("batch", "heads", "seq", None), P("heads", None, None),
            P("heads", None, None), P("heads", "seq"), P("seq"), P("seq", "heads"),
        ),
        out_specs=(P("batch", "seq"), P("batch", "heads"), P("batch")),
        check_vma=False,
    )
```

time: 203 us -> 84 us (0.41)
  waiting for transfers between devices: 91.1 us -> 0 us
  Pallas kernels: 0 us -> 71.6 us
  blocking collectives: 45 us -> 0 us
  starting transfers between devices: 28.4 us -> 0 us
  matrix products: 12.7 us -> 0 us
  local copies, waits for them, and re-layouts: 18.8 us -> 11.3 us
  other arithmetic: 5.18 us -> 0 us
    all_to_all x5 -> x0, waiting for transfers between devices: 91.1 us -> none  [the longest x4 76.2 us: copy_for_each(): lax.all_to_all(jnp.broadcast_to(value[None], (peers, *value.shape)), axis...]
    pallas_call x0 -> x1, Pallas kernels: none -> 71.6 us  [body(): pl.pallas_call(functools.partial(kernel, heads_size), name='decode_step',...]
    all_to_all x3 -> x0, blocking collectives: 45 us -> none  [copy_for_each(): lax.all_to_all(jnp.broadcast_to(value[None], (peers, *value.shape)), axis...]
    all_to_all x5 -> x0, starting transfers between devices: 28.4 us -> none  [the longest x4 24 us: copy_for_each(): lax.all_to_all(jnp.broadcast_to(value[None], (peers, *value.shape)), axis...]
    dot_general x9 -> x0, matrix products: 12.7 us -> none  [the longest x1 3.25 us: body(): jnp.dot((updated * final_gain).astype(jnp.bfloat16), w_vocab, preferred_e...]
    broadcast_in_dim x6 -> x0, local copies, waits for them, and re-layouts: 3.79 us -> none  [copy_for_each(): jnp.broadcast_to(value[None], (peers, *value.shape))]
    reduce_sum x9 -> x0, other arithmetic: 3.14 us -> none  [the longest x4 1.05 us: of_everyone(): return jnp.sum(everything, axis=0)]
    unnamed x28 -> x17, local copies, waits for them, and re-layouts: 10.8 us -> 9.38 us
  transfers between devices with their start and end apart: 5 -> 0, of which waited for: 5 -> 0; matrix products, arithmetic and copies ran while one was open for 7% -> 0% of each run, Pallas kernels for 0% -> 0%
where the time goes in v1:
time: 84 us; the launch traced here: 83.5 us
  Pallas kernels  71.6 us (85%)
  local copies, waits for them, and re-layouts  11.3 us (13%)
    pallas_call x1, Pallas kernels, body(): pl.pallas_call(functools.partial(kernel, heads_size), name='decode_step',...  71.6 us
    unnamed x17, local copies, waits for them, and re-layouts  9.38 us

profile of v1, /device:TPU:2, one launch (start us, length us, event | category | flops | bytes accessed | tf_op | source)
XLA Modules:
  0.0 83.5 jit_solution(4782543087692135346)
XLA Ops:
  0.6 0.7 reshape.24.gain
  1.3 0.7 reshape.29.fgain
  2.0 1.5 %copy.15.wo = bf16[1280,320]{1,0:T(8,128)(2,1)S(1)} copy(bf16[1280,320]{0,1:T(8,128)(2,1)} %param.21) | data formatting | bytes 1638400 | tf_op args[9]
  3.6 0.0 copy-start
  3.6 1.1 %copy-done = bf16[320,1280]{1,0:T(8,128)(2,1)S(1)} copy-done((bf16[320,1280]{1,0:T(8,128)(2,1)S(1)}, bf16[320,1280]{1,0:T(8,128)(2,1)}, u32[]{:S(2)}) %copy-start) | copy-done | bytes 819224
  4.7 0.0 copy-start.1
  4.7 1.1 %copy-done.1 = bf16[1,320,1280]{2,1,0:T(8,128)(2,1)S(1)} copy-done((bf16[1,320,1280]{2,1,0:T(8,128)(2,1)S(1)}, bf16[1,320,1280]{2,1,0:T(8,128)(2,1)}, u32[]{:S(2)}) %copy-start.1) | copy-done | bytes 819224
  5.8 0.0 copy-start.2
  5.8 1.1 %copy-done.2 = bf16[1,320,1280]{2,1,0:T(8,128)(2,1)S(1)} copy-done((bf16[1,320,1280]{2,1,0:T(8,128)(2,1)S(1)}, bf16[1,320,1280]{2,1,0:T(8,128)(2,1)}, u32[]{:S(2)}) %copy-start.2) | copy-done | bytes 819224
  7.0 0.0 copy-start.3
  7.0 1.0 %copy-done.3 = bf16[320,1,640]{2,0,1:T(8,128)(2,1)S(1)} copy-done((bf16[320,1,640]{2,0,1:T(8,128)(2,1)S(1)}, bf16[320,1,640]{2,0,1:T(8,128)(2,1)}, u32[]{:S(2)}) %copy-start.3) | copy-done | bytes 409624
  8.0 0.0 copy-start.4
  8.0 0.7 copy-done.4
  8.7 0.0 copy-start.5
  8.7 0.7 copy-done.5
  9.4 0.0 copy-start.6
  9.4 0.7 copy-done.6
  10.0 71.6 %decode_step.1 = (bf16[12,320]{1,0:T(8,128)(2,1)S(1)}, f32[12,8000]{1,0:T(8,128)S(1)}, f32[1,128]{1,0:T(1,128)S(1)}) custom-call(bf16[12,320]{1,0:T(8,128)(2,1)S(1)} %copy-done.4, s32[12]{0:T(128)S(1)} %copy-done.5, s32[12]{0:T(128)S(1)} %copy-done.6, f32[1,320]{1,0:T(1,128)S(1)} %reshape.24.gain, bf16[320,1280]{1,0:T(8,128)(2,1)S(1)} %copy-done, ...), custom_call_target="tpu_custom_call" | custom-call | tf_op jit(solution)/shard_map/decode_step/pallas_call | solution.py:513
  81.7 0.5 slice_bitcast_fusion
  82.2 0.6 copy.18
  82.8 0.8 copy.19
Async XLA Ops:
  3.6 1.1 %copy-start = (bf16[320,1280]{1,0:T(8,128)(2,1)S(1)}, bf16[320,1280]{1,0:T(8,128)(2,1)}, u32[]{:S(2)}) copy-start(bf16[320,1280]{1,0:T(8,128)(2,1)} %wq.1) | copy-start | bytes 2457604
  4.7 1.1 %copy-start.1 = (bf16[1,320,1280]{2,1,0:T(8,128)(2,1)S(1)}, bf16[1,320,1280]{2,1,0:T(8,128)(2,1)}, u32[]{:S(2)}) copy-start(bf16[1,320,1280]{2,1,0:T(8,128)(2,1)} %param.19) | copy-start | bytes 2457604
  5.8 1.1 %copy-start.2 = (bf16[1,320,1280]{2,1,0:T(8,128)(2,1)S(1)}, bf16[1,320,1280]{2,1,0:T(8,128)(2,1)}, u32[]{:S(2)}) copy-start(bf16[1,320,1280]{2,1,0:T(8,128)(2,1)} %param.20) | copy-start | bytes 2457604
  7.0 1.0 %copy-start.3 = (bf16[320,1,640]{2,0,1:T(8,128)(2,1)S(1)}, bf16[320,1,640]{2,0,1:T(8,128)(2,1)}, u32[]{:S(2)}) copy-start(bf16[320,1,640]{2,0,1:T(8,128)(2,1)} %param.17) | copy-start | bytes 1228804
  8.0 0.7 copy-start.4
  8.7 0.7 copy-start.5
  9.4 0.7 copy-start.6

commit v2 on v1

v2 whole, which is shorter than its diff:
```python
import functools
import math

import jax
import jax.numpy as jnp
from jax import lax
from jax.experimental import pallas as pl
from jax.experimental.pallas import tpu as pltpu
from jax.sharding import PartitionSpec as P

D = 5120
HEAD_DIM = 128
GROUP_HEADS = 10
RANK = 320
SEQ = 16
ROWS = 12
SPAN = 256
WIDE = 512
VOCAB_LOCAL = 8000
PIECES = 15
TAIL = VOCAB_LOCAL - 15 * WIDE

MESH = pl.DeviceIdType.MESH
f32 = jnp.float32
bf16 = jnp.bfloat16
epsilon = 1e-05
negative_fill = -1e30
scaling = 1.0 / math.sqrt(HEAD_DIM)

QUERY_SUM, QUERY_ALL, HEAD_SUM, HEAD_ALL, SQUARES, VOCAB_SUM, VOCAB_ALL, STATS = range(8)


def owner_of_head(k):
    return lax.div(k * 8, 5)


def head_of_owner(s):
    return lax.div(s * 5 + 7, 8)


def owns_head(s):
    return owner_of_head(head_of_owner(s)) == s


def iota(shape, dim):
    return lax.broadcasted_iota(jnp.int32, shape, dim)


def as_row(column):
    spread = jnp.where(iota((16, 128), 0) == iota((16, 128), 1), column, 0.0)
    return jnp.sum(spread, axis=0, keepdims=True)


def as_column(row, picks):
    return jnp.sum(jnp.where(picks == iota(picks.shape, 1), row, 0.0), axis=1, keepdims=True)


def kernel(
    heads_size,
    hidden, lengths, drafts, gain, wq, wl, cache, ku, vu, wo, fgain, wv,
    new_hidden, vd_all, logs_out, draft_out,
    hid_v, len_s, draft_s, gain_v, wq_v, wl_v, cache_v, ku_v, vu_v, wo_v, fgain_v, wv_v,
    states_v,
    qa_send, qa_recv, qa_all,
    absorbed_v, mixed_v,
    hb_send, hb_recv, hb_all, own_v,
    at_send, at_recv,
    sq_send, sq_recv,
    vd_send, vd_recv,
    st_send, st_recv,
    load_sem, send_sem, recv_sem, x_send_sem, x_recv_sem,
):
    me = lax.axis_index("seq")
    hme = lax.axis_index("heads")

    def peer_at(j):
        t = lax.div(j, 2)
        over_z = 4 + (1 - 2 * lax.rem(t, 2)) * lax.div(t + 1, 2)
        y, z = lax.div(me, 8), lax.rem(me, 8)
        return lax.rem(y + 1 - lax.rem(j, 2), 2) * 8 + lax.rem(z + over_z, 8)

    def each_peer(step, start=0, stop=SEQ - 1):
        @pl.loop(start, stop)
        def _(j):
            step(peer_at(j))

    barrier = pltpu.get_barrier_semaphore()

    @each_peer
    def _(peer):
        pl.semaphore_signal(barrier, inc=1, device_id={"seq": peer}, device_id_type=MESH)

    for j in range(1, heads_size):
        pl.semaphore_signal(
            barrier, inc=1, device_id={"heads": lax.rem(hme + j, heads_size)}, device_id_type=MESH
        )

    loads = [
        (hidden, hid_v), (gain, gain_v), (lengths, len_s), (drafts, draft_s), (fgain, fgain_v),
        (wq, wq_v), (wl, wl_v), (ku, ku_v), (cache, cache_v), (vu, vu_v.at[pl.ds(64, RANK)]),
        (wo, wo_v), (wv, wv_v),
    ]
    loads = [pltpu.make_async_copy(a, b, load_sem.at[i]) for i, (a, b) in enumerate(loads)]
    l_hid, l_gain, l_len, l_draft, l_fgain, l_wq, l_wl, l_ku, l_cache, l_vu, l_wo, l_wv = loads
    for load in loads:
        load.start()

    def over_seq(phase, src, dst, peer):
        return pltpu.make_async_remote_copy(
            src_ref=src, dst_ref=dst,
            send_sem=send_sem.at[phase], recv_sem=recv_sem.at[phase],
            device_id={"seq": peer}, device_id_type=MESH,
        )

    def arrived(phase, ref, count):
        ref = ref.at[pl.ds(0, count)]
        pltpu.make_async_copy(ref, ref, recv_sem.at[phase]).wait()

    def sent(phase, ref, count):
        ref = ref.at[pl.ds(0, count)]
        pltpu.make_async_copy(ref, ref, send_sem.at[phase]).wait()

    def either(phase, ref, condition, count, waits):
        @pl.when(condition)
        def _():
            waits(phase, ref, count - ref_rows(ref))

        @pl.when(jnp.logical_not(condition))
        def _():
            waits(phase, ref, count)

    def ref_rows(ref):
        return 16 if len(ref.shape) == 2 else 1

    def rows16(ref, i):
        return ref.at[pl.ds(pl.multiple_of(i * 16, 16), 16)]

    vu_v[0:64, :] = jnp.zeros((64, GROUP_HEADS * HEAD_DIM), bf16)
    absorbed_v[...] = jnp.zeros_like(absorbed_v)
    mixed_v[...] = jnp.zeros_like(mixed_v)
    states_v[...] = jnp.zeros_like(states_v)
    l_hid.wait()
    l_gain.wait()
    states_v[0:ROWS, :] = hid_v[...].astype(f32)
    states = states_v[...]
    gained = (states * gain_v[...].reshape(1, RANK)).astype(bf16)
    squares = as_row(jnp.sum(states * states, axis=1, keepdims=True))
    row = iota((16, 128), 0)
    l_wq.wait()
    query_part = jnp.dot(gained, wq_v[...], preferred_element_type=f32)
    for k in range(10):
        part = query_part[:, k * 128 : (k + 1) * 128]
        qa_send[k * 16 : (k + 1) * 16, :] = jnp.where(row == 12, squares, part)
    l_wl.wait()
    latent_part = jnp.dot(gained, wl_v[...], preferred_element_type=f32)
    for k in range(5):
        part = latent_part[:, k * 128 : (k + 1) * 128]
        qa_send[(k + 10) * 16 : (k + 11) * 16, :] = jnp.where(row == 12, squares, part)

    pl.semaphore_wait(barrier, SEQ - 1 + heads_size - 1)

    @each_peer
    def _(peer):
        @pl.when(peer < PIECES)
        def _():
            over_seq(QUERY_SUM, rows16(qa_send, peer), rows16(qa_recv, me), peer).start()

    @pl.when(me < PIECES)
    def _():
        qa_recv[pl.ds(pl.multiple_of(me * 16, 16), 16), :] = qa_send[
            pl.ds(pl.multiple_of(me * 16, 16), 16), :
        ]

        arrived(QUERY_SUM, qa_recv, 15 * 16)

        total = qa_recv[0:16, :]
        for i in range(1, SEQ):
            total = total + qa_recv[i * 16 : (i + 1) * 16, :]
        mean = as_column(total[12:13, :], row) / D
        done = (lax.rsqrt(mean + epsilon) * total).astype(bf16).astype(f32)
        qa_all[pl.ds(pl.multiple_of(me * 16, 16), 16), :] = jnp.where(row < ROWS, done, 0.0)

        @each_peer
        def _(peer):
            over_seq(QUERY_ALL, rows16(qa_all, me), rows16(qa_all, me), peer).start()

    either(QUERY_ALL, qa_all, me < PIECES, PIECES * 16, arrived)

    l_ku.wait()
    for k in range(GROUP_HEADS):
        query = qa_all[k * 16 : (k + 1) * 16, :].astype(bf16)
        absorbed = lax.dot_general(
            query, ku_v[:, k * 128 : (k + 1) * 128], (((1,), (1,)), ((), ())),
            preferred_element_type=f32,
        )
        absorbed = absorbed.astype(bf16).astype(f32)
        absorbed_v[0, k * 16 : (k + 1) * 16, :] = absorbed[:, 0:128]
        absorbed_v[1, k * 16 : (k + 1) * 16, :] = absorbed[:, 128:256]
        absorbed_v[2, k * 16 : (k + 1) * 16, 0:64] = absorbed[:, 256:320]

    l_len.wait()
    l_cache.wait()
    positions = me * SPAN + iota((16, SPAN), 1)
    lane = iota((16, 128), 1)
    maxima = jnp.zeros((16, 128), f32)
    totals = jnp.zeros((16, 128), f32)
    scores = []
    for b in range(ROWS):
        one = jnp.concatenate(
            [absorbed_v[t, pl.ds(b, 16, stride=16), :] for t in range(3)], axis=1
        ).astype(bf16)
        scores.append(
            lax.dot_general(
                one, cache_v[b, :, 0:384], (((1,), (1,)), ((), ())), preferred_element_type=f32
            )
        )
    weights = []
    for b in range(ROWS):
        live = positions < len_s[b]
        score = jnp.where(live, scores[b] * scaling, negative_fill)
        top = jnp.max(score, axis=1, keepdims=True)
        weight = jnp.where(live, jnp.exp(score - top), 0.0)
        maxima = jnp.where(lane == b, top, maxima)
        totals = jnp.where(lane == b, jnp.sum(weight, axis=1, keepdims=True), totals)
        weights.append(weight.astype(bf16))
    for b in range(ROWS):
        mixed = jnp.dot(weights[b], cache_v[b, :, 256:640], preferred_element_type=f32)
        for t in range(3):
            mixed_v[t, b * 16 : (b + 1) * 16, :] = mixed[:, t * 128 : (t + 1) * 128]

    l_vu.wait()
    for k in range(GROUP_HEADS):
        mixed = jnp.concatenate(
            [mixed_v[t, pl.ds(k, 16, stride=16), :] for t in range(3)], axis=1
        )
        high = mixed.astype(bf16)
        low = (mixed - high.astype(f32)).astype(bf16)
        both = jnp.dot(
            jnp.concatenate([high, low], axis=0), vu_v[:, k * 128 : (k + 1) * 128],
            preferred_element_type=f32,
        )
        part = both[0:16] + both[16:32]
        part = jnp.where(row == 12, maxima[k : k + 1, :], part)
        part = jnp.where(row == 13, totals[k : k + 1, :], part)
        hb_send[k * 16 : (k + 1) * 16, :] = part

    @each_peer
    def _(peer):
        @pl.when(owns_head(peer))
        def _():
            over_seq(
                HEAD_SUM, rows16(hb_send, head_of_owner(peer)), rows16(hb_recv, me), peer
            ).start()

    own_key = jnp.concatenate([qa_all[(10 + t) * 16 : (11 + t) * 16, :] for t in range(3)], axis=1)
    own_value = jnp.concatenate(
        [qa_all[(12 + t) * 16 : (13 + t) * 16, :] for t in range(3)], axis=1
    ).astype(bf16)
    own = jnp.dot(own_value, vu_v[...], preferred_element_type=f32)
    for k in range(GROUP_HEADS):
        own_v[k * 16 : (k + 1) * 16, :] = own[:, k * 128 : (k + 1) * 128]

    @pl.when(owns_head(me))
    def _():
        k = head_of_owner(me)
        mine = pl.ds(pl.multiple_of(k * 16, 16), 16)
        hb_recv[pl.ds(pl.multiple_of(me * 16, 16), 16), :] = hb_send[mine, :]
        absorbed = jnp.concatenate([absorbed_v[t, mine, :] for t in range(3)], axis=1)
        own_score = jnp.sum(absorbed * own_key, axis=1, keepdims=True) * scaling

        arrived(HEAD_SUM, hb_recv, 15 * 16)

        tops = hb_recv[pl.ds(12, 16, stride=16), :].T[0:16, :]
        sums = hb_recv[pl.ds(13, 16, stride=16), :].T[0:16, :]
        highest = jnp.maximum(jnp.max(tops, axis=1, keepdims=True), own_score)
        shares = jnp.exp(tops - highest)
        own_weight = jnp.exp(own_score - highest)
        denominator = jnp.sum(shares * sums, axis=1, keepdims=True) + own_weight
        total = own_weight * own_v[mine, :]
        for i in range(SEQ):
            total = total + shares[:, i : i + 1] * hb_recv[i * 16 : (i + 1) * 16, :]
        head_out = (total / denominator).astype(bf16).astype(f32)
        hb_all[mine, :] = jnp.where(row < ROWS, head_out, 0.0)

        @each_peer
        def _(peer):
            over_seq(HEAD_ALL, rows16(hb_all, k), rows16(hb_all, k), peer).start()

    either(HEAD_ALL, hb_all, owns_head(me), GROUP_HEADS * 16, arrived)

    def over_heads(src, dst, peer):
        return pltpu.make_async_remote_copy(
            src_ref=src, dst_ref=dst,
            send_sem=x_send_sem.at[peer], recv_sem=x_recv_sem.at[hme],
            device_id={"heads": peer}, device_id_type=MESH,
        )

    l_wo.wait()
    heads_out = jnp.concatenate(
        [hb_all[k * 16 : (k + 1) * 16, :] for k in range(GROUP_HEADS)], axis=1
    ).astype(bf16)
    at_send[...] = lax.dot_general(
        heads_out, wo_v[...], (((1,), (1,)), ((), ())), preferred_element_type=f32
    )
    for j in range(1, heads_size):
        peer = lax.rem(hme + j, heads_size)
        over_heads(at_send, at_recv.at[hme], peer).start()
    at_recv[hme] = at_send[...]
    l_fgain.wait()
    for j in range(1, heads_size):
        peer = lax.rem(hme + j, heads_size)
        pltpu.make_async_copy(at_send, at_send, x_recv_sem.at[peer]).wait()
    attn = at_recv[0]
    for h in range(1, heads_size):
        attn = attn + at_recv[h]
    updated = states_v[...] + attn
    new_hidden[...] = updated[0:ROWS].astype(bf16)
    sq_send[...] = as_row(jnp.sum(updated * updated, axis=1, keepdims=True))

    @each_peer
    def _(peer):
        over_seq(SQUARES, sq_send, sq_recv.at[me], peer).start()

    scaled = updated * fgain_v[...].reshape(1, RANK)
    bottom = scaled[8:16]
    bottom = jnp.where(iota(bottom.shape, 0) < 4, bottom, pltpu.roll(bottom, 4, 0))
    twice = jnp.concatenate([scaled[0:8], bottom], axis=0).astype(bf16)
    l_wv.wait()
    lower = iota((8, 256), 0) < 4

    def piece(c):
        terms = jnp.dot(
            twice, wv_v[:, pl.ds(pl.multiple_of(c * WIDE, WIDE), WIDE)], preferred_element_type=f32
        )
        vd_send[c, :, 0:512] = terms[0:8]
        vd_send[c, :, 512:768] = jnp.where(lower, terms[8:16, 0:256], terms[8:16, 256:512])

    def last_piece():
        terms = jnp.dot(twice, wv_v[:, 15 * WIDE : VOCAB_LOCAL], preferred_element_type=f32)
        vd_send[15] = jnp.zeros((8, 768), f32)
        vd_send[15, :, 0:TAIL] = terms[0:8]
        vd_send[15, 0:4, 512:768] = terms[8:12, 0:256]
        vd_send[15, 4:8, 512 : 512 + TAIL - 256] = terms[12:16, 256:TAIL]

    def any_piece(c):
        @pl.when(c < 15)
        def _():
            piece(c)

        @pl.when(c == 15)
        def _():
            last_piece()

    @each_peer
    def _(peer):
        any_piece(peer)
        over_seq(VOCAB_SUM, vd_send.at[peer], vd_recv.at[me], peer).start()

    any_piece(me)
    vd_recv[me] = vd_send[me]
    sq_recv[me] = sq_send[...]

    arrived(SQUARES, sq_recv, 15)
    arrived(VOCAB_SUM, vd_recv, 15)

    square_total = sq_recv[0]
    share = vd_recv[0]
    for i in range(1, SEQ):
        square_total = square_total + sq_recv[i]
        share = share + vd_recv[i]
    inv = lax.rsqrt(square_total / D + epsilon)
    sub = iota((8, 128), 0)
    inv_top = as_column(inv, sub)
    inv_bottom = as_column(inv, 8 + lax.rem(sub, 4))
    spot = iota((8, 512), 1)
    spot_bottom = iota((8, 256), 1) + jnp.where(lower, 0, 256)
    limit = VOCAB_LOCAL - me * WIDE
    vd_all[me, :, 0:512] = jnp.where(spot < limit, share[:, 0:512] * inv_top, negative_fill)
    vd_all[me, :, 512:768] = jnp.where(
        spot_bottom < limit, share[:, 512:768] * inv_bottom, negative_fill
    )

    def send_logits(peer):
        over_seq(VOCAB_ALL, vd_all.at[me], vd_all.at[me], peer).start()

    each_peer(send_logits, 0, 4)

    l_draft.wait()
    sub1 = iota((8, 1), 0)
    draft_top = jnp.zeros((8, 1), jnp.int32)
    draft_bottom = jnp.zeros((8, 1), jnp.int32)
    for b in range(8):
        draft_top = jnp.where(sub1 == b, draft_s[b], draft_top)
    for b in range(4):
        draft_bottom = jnp.where(lax.rem(sub1, 4) == b, draft_s[8 + b], draft_bottom)
    first = hme * VOCAB_LOCAL + me * WIDE
    draft_top = draft_top - first
    draft_bottom = draft_bottom - first

    def other_half(column):
        return pltpu.roll(jnp.broadcast_to(column, (8, 128)), 4, 0)[:, 0:1]

    high = vd_all[me, :, 0:512]
    low = vd_all[me, :, 512:768]
    max_top = jnp.max(high, axis=1, keepdims=True)
    max_bottom = jnp.max(low, axis=1, keepdims=True)
    max_bottom = jnp.maximum(max_bottom, other_half(max_bottom))
    sum_top = jnp.sum(jnp.exp(high - max_top), axis=1, keepdims=True)
    sum_bottom = jnp.sum(jnp.exp(low - max_bottom), axis=1, keepdims=True)
    sum_bottom = sum_bottom + other_half(sum_bottom)
    pick_top = jnp.sum(
        jnp.where((spot == draft_top) & (spot < limit), high, 0.0), axis=1, keepdims=True
    )
    pick_bottom = jnp.sum(
        jnp.where((spot_bottom == draft_bottom) & (spot_bottom < limit), low, 0.0),
        axis=1, keepdims=True,
    )
    pick_bottom = pick_bottom + other_half(pick_bottom)

    lane8 = iota((8, 128), 1)
    block = jnp.zeros((8, 128), f32)
    for i, (upper, under) in enumerate(
        ((max_top, max_bottom), (sum_top, sum_bottom), (pick_top, pick_bottom))
    ):
        block = jnp.where(lane8 == sub + 16 * i, upper, block)
        block = jnp.where((lane8 == sub + 16 * i + 8) & (sub < 4), under, block)
    stats = jnp.sum(block, axis=0, keepdims=True)
    st_send[...] = stats
    slot = hme * SEQ + me
    st_recv[slot] = stats

    def send_stats(peer, j):
        pltpu.make_async_remote_copy(
            src_ref=st_send, dst_ref=st_recv.at[slot],
            send_sem=send_sem.at[STATS], recv_sem=recv_sem.at[STATS],
            device_id={"seq": peer, "heads": lax.rem(hme + j, heads_size)}, device_id_type=MESH,
        ).start()

    @each_peer
    def _(peer):
        for j in range(heads_size):
            send_stats(peer, j)

    for j in range(1, heads_size):
        send_stats(me, j)

    each_peer(send_logits, 4, SEQ - 1)

    either(QUERY_SUM, qa_send, me < PIECES, PIECES * 16, sent)

    @pl.when(me < PIECES)
    def _():
        sent(QUERY_ALL, qa_recv, 15 * 16)

    either(HEAD_SUM, hb_send, owns_head(me), GROUP_HEADS * 16, sent)

    @pl.when(owns_head(me))
    def _():
        sent(HEAD_ALL, hb_recv, 15 * 16)

    sent(SQUARES, sq_recv, 15)
    sent(VOCAB_SUM, vd_send, 15)
    for j in range(1, heads_size):
        peer = lax.rem(hme + j, heads_size)
        pltpu.make_async_copy(at_send, at_send, x_send_sem.at[peer]).wait()

    arrived(VOCAB_ALL, vd_all, 15)
    arrived(STATS, st_recv, heads_size * SEQ - 1)
    every = [st_recv[i] for i in range(heads_size * SEQ)]
    highest = functools.reduce(jnp.maximum, every)
    total = jnp.zeros((1, 128), f32)
    picked = jnp.zeros((1, 128), f32)
    for one in every:
        total = total + jnp.exp(one - highest) * pltpu.roll(one, 112, 1)
        picked = picked + one
    log_total = highest + jnp.log(jnp.where(lane8[0:1] < ROWS, total, 1.0))
    draft_out[...] = pltpu.roll(picked, 96, 1) - log_total
    log_top = as_column(log_total, sub)
    log_bottom = as_column(log_total, 8 + lax.rem(sub, 4))
    logs_out[...] = jnp.where(lane8 == 0, log_top, log_bottom)
    sent(VOCAB_ALL, vd_recv, 15)
    sent(STATS, st_recv, heads_size * SEQ - 1)


def closing_kernel(
    new_hidden, logits, logs, draft, hidden_out, probs_out, draft_out, upper_v, lower_v, draft_v, sem
):
    copies = [
        pltpu.make_async_copy(new_hidden, hidden_out, sem.at[0]),
        pltpu.make_async_copy(draft_v, draft_out, sem.at[1]),
        pltpu.make_async_copy(upper_v, probs_out.at[pl.ds(0, 8)], sem.at[2]),
        pltpu.make_async_copy(lower_v, probs_out.at[pl.ds(8, 4)], sem.at[3]),
    ]
    copies[0].start()
    draft_v[...] = draft[...].reshape(128)[:ROWS]
    copies[1].start()
    log_top, log_bottom = logs[:, 0:1], logs[:, 1:2]
    for c in range(SEQ):
        at = c * WIDE
        width = min(WIDE, VOCAB_LOCAL - at)
        upper_v[:, at : at + width] = logits[c, :, 0:width] - log_top
    copies[2].start()
    for c in range(SEQ):
        at = c * WIDE
        low = logits[c, :, 512:768] - log_bottom
        lower_v[:, at : at + 256] = low[0:4]
        rest = min(256, VOCAB_LOCAL - at - 256)
        lower_v[:, at + 256 : at + 256 + rest] = pltpu.roll(low, 4, 0)[0:4, 0:rest]
    copies[3].start()
    for copy in copies:
        copy.wait()


def solution(mesh):
    heads_size = mesh.shape["heads"]

    def body(hidden, lengths, drafts, gain, wq, wl, cache, ku, vu, wo, fgain, wv):
        hbm = pl.BlockSpec(memory_space=pltpu.HBM)
        vmem = pl.BlockSpec(memory_space=pltpu.VMEM)
        width = GROUP_HEADS * HEAD_DIM
        results = pl.pallas_call(
            functools.partial(kernel, heads_size),
            name="decode_step",
            out_shape=(
                jax.ShapeDtypeStruct((ROWS, RANK), bf16),
                jax.ShapeDtypeStruct((SEQ, 8, 768), f32),
                jax.ShapeDtypeStruct((8, 128), f32),
                jax.ShapeDtypeStruct((1, 128), f32),
            ),
            in_specs=[hbm] * 12,
            out_specs=(vmem,) * 4,
            scratch_shapes=[
                pltpu.VMEM((ROWS, RANK), bf16),
                pltpu.SMEM((ROWS,), jnp.int32),
                pltpu.SMEM((ROWS,), jnp.int32),
                pltpu.VMEM((RANK,), f32),
                pltpu.VMEM((RANK, width), bf16),
                pltpu.VMEM((RANK, 2 * RANK), bf16),
                pltpu.VMEM((ROWS, SPAN, 2 * RANK), bf16),
                pltpu.VMEM((RANK, width), bf16),
                pltpu.VMEM((384, width), bf16),
                pltpu.VMEM((RANK, width), bf16),
                pltpu.VMEM((RANK,), f32),
                pltpu.VMEM((RANK, VOCAB_LOCAL), bf16),
                pltpu.VMEM((16, RANK), f32),
                pltpu.VMEM((256, 128), f32),
                pltpu.VMEM((256, 128), f32),
                pltpu.VMEM((256, 128), f32),
                pltpu.VMEM((3, 256, 128), f32),
                pltpu.VMEM((3, 256, 128), f32),
                pltpu.VMEM((160, 128), f32),
                pltpu.VMEM((256, 128), f32),
                pltpu.VMEM((160, 128), f32),
                pltpu.VMEM((160, 128), f32),
                pltpu.VMEM((16, RANK), f32),
                pltpu.VMEM((heads_size, 16, RANK), f32),
                pltpu.VMEM((1, 128), f32),
                pltpu.VMEM((SEQ, 1, 128), f32),
                pltpu.VMEM((SEQ, 8, 768), f32),
                pltpu.VMEM((SEQ, 8, 768), f32),
                pltpu.VMEM((1, 128), f32),
                pltpu.VMEM((heads_size * SEQ, 1, 128), f32),
                pltpu.SemaphoreType.DMA((12,)),
                pltpu.SemaphoreType.DMA((8,)),
                pltpu.SemaphoreType.DMA((8,)),
                pltpu.SemaphoreType.DMA((heads_size,)),
                pltpu.SemaphoreType.DMA((heads_size,)),
            ],
            compiler_params=pltpu.CompilerParams(
                collective_id=0, has_side_effects=True, vmem_limit_bytes=48 * 1024 * 1024
            ),
        )(*(pltpu.with_memory_space_constraint(x, pltpu.HBM) for x in (
            hidden, lengths, drafts, gain, wq, wl.reshape(RANK, 2 * RANK),
            cache.reshape(ROWS, SPAN, 2 * RANK), ku.reshape(RANK, width), vu.reshape(RANK, width),
            wo.T, fgain, wv,
        )))
        return pl.pallas_call(
            closing_kernel,
            name="outputs",
            out_shape=(
                jax.ShapeDtypeStruct((ROWS, RANK), bf16),
                jax.ShapeDtypeStruct((ROWS, VOCAB_LOCAL), f32),
                jax.ShapeDtypeStruct((ROWS,), f32),
            ),
            in_specs=[vmem] * 4,
            out_specs=(hbm,) * 3,
            scratch_shapes=[
                pltpu.VMEM((8, VOCAB_LOCAL), f32),
                pltpu.VMEM((4, VOCAB_LOCAL), f32),
                pltpu.VMEM((ROWS,), f32),
                pltpu.SemaphoreType.DMA((4,)),
            ],
            compiler_params=pltpu.CompilerParams(vmem_limit_bytes=4 * 1024 * 1024),
        )(*results)

    return jax.shard_map(
        body,
        mesh=mesh,
        in_specs=(
            P("batch", "seq"), P("batch"), P("batch"), P("seq"), P("seq", "heads"),
            P("seq", "heads", None), P("batch", "heads", "seq", None), P("heads", None, None),
            P("heads", None, None), P("heads", "seq"), P("seq"), P("seq", "heads"),
        ),
        out_specs=(P("batch", "seq"), P("batch", "heads"), P("batch")),
        check_vma=False,
    )
```

time: 84 us -> 63.9 us (0.76)
  local copies, waits for them, and re-layouts: 11.3 us -> 0 us
  Pallas kernels: 71.6 us -> 63.1 us
    pallas_call x1, Pallas kernels: 71.6 us -> 62.2 us  [body(): pl.pallas_call(functools.partial(kernel, heads_size), name='decode_step',...]
    unnamed x17 -> x0, local copies, waits for them, and re-layouts: 9.38 us -> none
    reshape x2 -> x0, local copies, waits for them, and re-layouts: 1.37 us -> none  [the longest x1 0.68 us: body(): gain.reshape(1, RANK)]
    pallas_call x0 -> x1, Pallas kernels: none -> 0.87 us  [body(): pl.pallas_call(closing_kernel, name='outputs', out_shape=(jax.ShapeDtypeS...]
where the time goes in v2:
time: 63.9 us; the launch traced here: 63.7 us
  Pallas kernels  63.1 us (99%)
  between operations  0.64 us (1%)
    pallas_call x1, Pallas kernels, body(): pl.pallas_call(functools.partial(kernel, heads_size), name='decode_step',...  62.2 us

profile of v2, /device:TPU:2, one launch (start us, length us, event | category | flops | bytes accessed | tf_op | source)
XLA Modules:
  0.0 63.7 jit_solution(17234960723600553974)
XLA Ops:
  0.6 62.2 %decode_step.1 = (bf16[12,320]{1,0:T(8,128)(2,1)S(1)}, f32[16,8,768]{2,1,0:T(8,128)S(1)}, f32[8,128]{1,0:T(8,128)S(1)}, f32[1,128]{1,0:T(1,128)S(1)}) custom-call(bf16[12,320]{1,0:T(8,128)(2,1)} %hidden.1, s32[12]{0:T(128)} %lengths.1, s32[12]{0:T(128)} %drafts.1, f32[320]{0:T(512)} %gain.1, bf16[320,1280]{1,0:T(8,128)(2,1)} %wq.1, ...), custom_call_target="tpu_custom_call" | custom-call | tf_op jit(solution)/shard_map/decode_step/pallas_call | solution.py:521
  62.9 0.9 %outputs.1 = (bf16[12,320]{1,0:T(8,128)(2,1)}, f32[12,8000]{1,0:T(8,128)}, f32[12]{0:T(128)}) custom-call(bf16[12,320]{1,0:T(8,128)(2,1)S(1)} %get-tuple-element.7.new_hidden, f32[16,8,768]{2,1,0:T(8,128)S(1)} %get-tuple-element.8.logits, f32[8,128]{1,0:T(8,128)S(1)} %get-tuple-element.9.logs, f32[1,128]{1,0:T(1,128)S(1)} %get-tuple-element.10.draft), custom_call_target="tpu_custom_call" | custom-call | tf_op jit(solution)/shard_map/outputs/pallas_call | solution.py:577

commit v3 on v2

--- a/solution.py
+++ b/solution.py
@@ -68,10 +68,13 @@
     sq_send, sq_recv,
     vd_send, vd_recv,
     st_send, st_recv,
-    load_sem, send_sem, recv_sem, x_send_sem, x_recv_sem,
+    load_sem, send_sem, recv_sem, x_send_sem, x_recv_sem, turn_sem,
 ):
     me = lax.axis_index("seq")
     hme = lax.axis_index("heads")
+    batch = lax.axis_index("batch")
+    core = lax.rem(batch, 2)
+    partner = batch + 1 - 2 * core
 
     def peer_at(j):
         t = lax.div(j, 2)
@@ -90,6 +93,7 @@
     def _(peer):
         pl.semaphore_signal(barrier, inc=1, device_id={"seq": peer}, device_id_type=MESH)
 
+    pl.semaphore_signal(barrier, inc=1, device_id={"batch": partner}, device_id_type=MESH)
     for j in range(1, heads_size):
         pl.semaphore_signal(
             barrier, inc=1, device_id={"heads": lax.rem(hme + j, heads_size)}, device_id_type=MESH
@@ -157,7 +161,7 @@
         part = latent_part[:, k * 128 : (k + 1) * 128]
         qa_send[(k + 10) * 16 : (k + 11) * 16, :] = jnp.where(row == 12, squares, part)
 
-    pl.semaphore_wait(barrier, SEQ - 1 + heads_size - 1)
+    pl.semaphore_wait(barrier, SEQ + heads_size - 1)
 
     @each_peer
     def _(peer):
@@ -360,6 +364,11 @@
     vd_recv[me] = vd_send[me]
     sq_recv[me] = sq_send[...]
 
+    @pl.when(core == 0)
+    def _():
+        sent(VOCAB_SUM, vd_send, 15)
+        pl.semaphore_signal(turn_sem, inc=1, device_id={"batch": partner}, device_id_type=MESH)
+
     arrived(SQUARES, sq_recv, 15)
     arrived(VOCAB_SUM, vd_recv, 15)
 
@@ -380,6 +389,10 @@
         spot_bottom < limit, share[:, 512:768] * inv_bottom, negative_fill
     )
 
+    @pl.when(core == 1)
+    def _():
+        pl.semaphore_wait(turn_sem, 1)
+
     def send_logits(peer):
         over_seq(VOCAB_ALL, vd_all.at[me], vd_all.at[me], peer).start()
 
@@ -459,7 +472,11 @@
         sent(HEAD_ALL, hb_recv, 15 * 16)
 
     sent(SQUARES, sq_recv, 15)
-    sent(VOCAB_SUM, vd_send, 15)
+
+    @pl.when(core == 1)
+    def _():
+        sent(VOCAB_SUM, vd_send, 15)
+
     for j in range(1, heads_size):
         peer = lax.rem(hme + j, heads_size)
         pltpu.make_async_copy(at_send, at_send, x_send_sem.at[peer]).wait()
@@ -565,6 +582,7 @@
                 pltpu.SemaphoreType.DMA((8,)),
                 pltpu.SemaphoreType.DMA((heads_size,)),
                 pltpu.SemaphoreType.DMA((heads_size,)),
+                pltpu.SemaphoreType.REGULAR,
             ],
             compiler_params=pltpu.CompilerParams(
                 collective_id=0, has_side_effects=True, vmem_limit_bytes=48 * 1024 * 1024

time: 63.9 us -> 61.2 us (0.958)
  Pallas kernels: 63.1 us -> 59.9 us
    pallas_call x1, Pallas kernels: 62.2 us -> 59 us  [body(): pl.pallas_call(functools.partial(kernel, heads_size), name='decode_step',...]
where the time goes in v3:
time: 61.2 us; the launch traced here: 60.5 us
  Pallas kernels  59.9 us (98%)
  between operations  0.64 us (1%)
    pallas_call x1, Pallas kernels, body(): pl.pallas_call(functools.partial(kernel, heads_size), name='decode_step',...  59 us

profile of v3, /device:TPU:2, one launch (start us, length us, event | category | flops | bytes accessed | tf_op | source)
XLA Modules:
  0.0 60.5 jit_solution(5976143477516647754)
XLA Ops:
  0.6 59.0 %decode_step.1 = (bf16[12,320]{1,0:T(8,128)(2,1)S(1)}, f32[16,8,768]{2,1,0:T(8,128)S(1)}, f32[8,128]{1,0:T(8,128)S(1)}, f32[1,128]{1,0:T(1,128)S(1)}) custom-call(bf16[12,320]{1,0:T(8,128)(2,1)} %hidden.1, s32[12]{0:T(128)} %lengths.1, s32[12]{0:T(128)} %drafts.1, f32[320]{0:T(512)} %gain.1, bf16[320,1280]{1,0:T(8,128)(2,1)} %wq.1, ...), custom_call_target="tpu_custom_call" | custom-call | tf_op jit(solution)/shard_map/decode_step/pallas_call | solution.py:538
  59.7 0.9 %outputs.1 = (bf16[12,320]{1,0:T(8,128)(2,1)}, f32[12,8000]{1,0:T(8,128)}, f32[12]{0:T(128)}) custom-call(bf16[12,320]{1,0:T(8,128)(2,1)S(1)} %get-tuple-element.7.new_hidden, f32[16,8,768]{2,1,0:T(8,128)S(1)} %get-tuple-element.8.logits, f32[8,128]{1,0:T(8,128)S(1)} %get-tuple-element.9.logs, f32[1,128]{1,0:T(1,128)S(1)} %get-tuple-element.10.draft), custom_call_target="tpu_custom_call" | custom-call | tf_op jit(solution)/shard_map/outputs/pallas_call | solution.py:595

commit v4 on v3

--- a/solution.py
+++ b/solution.py
@@ -18,6 +18,7 @@
 WIDE = 512
 VOCAB_LOCAL = 8000
 PIECES = 15
+NEAR = 3
 TAIL = VOCAB_LOCAL - 15 * WIDE
 
 MESH = pl.DeviceIdType.MESH
@@ -27,7 +28,7 @@
 negative_fill = -1e30
 scaling = 1.0 / math.sqrt(HEAD_DIM)
 
-QUERY_SUM, QUERY_ALL, HEAD_SUM, HEAD_ALL, SQUARES, VOCAB_SUM, VOCAB_ALL, STATS = range(8)
+QUERY_SUM, QUERY_ALL, HEAD_SUM, HEAD_ALL, SQUARES, VOCAB_SUM, VOCAB_ALL, STATS, VOCAB_HALF = range(9)
 
 
 def owner_of_head(k):
@@ -66,9 +67,9 @@
     hb_send, hb_recv, hb_all, own_v,
     at_send, at_recv,
     sq_send, sq_recv,
-    vd_send, vd_recv,
+    vd_send, vd_recv, vd_half,
     st_send, st_recv,
-    load_sem, send_sem, recv_sem, x_send_sem, x_recv_sem, turn_sem,
+    load_sem, send_sem, recv_sem, x_send_sem, x_recv_sem, turn_sem, near_sem, half_sem,
 ):
     me = lax.axis_index("seq")
     hme = lax.axis_index("heads")
@@ -124,20 +125,17 @@
         ref = ref.at[pl.ds(0, count)]
         pltpu.make_async_copy(ref, ref, send_sem.at[phase]).wait()
 
-    def either(phase, ref, condition, count, waits):
+    def rows(ref, i, count):
+        return ref.at[pl.ds(pl.multiple_of(i * 16, 16), count)]
+
+    def either(phase, ref, condition, count, size, waits):
         @pl.when(condition)
         def _():
-            waits(phase, ref, count - ref_rows(ref))
+            waits(phase, ref, (count - 1) * size)
 
         @pl.when(jnp.logical_not(condition))
         def _():
-            waits(phase, ref, count)
-
-    def ref_rows(ref):
-        return 16 if len(ref.shape) == 2 else 1
-
-    def rows16(ref, i):
-        return ref.at[pl.ds(pl.multiple_of(i * 16, 16), 16)]
+            waits(phase, ref, count * size)
 
     vu_v[0:64, :] = jnp.zeros((64, GROUP_HEADS * HEAD_DIM), bf16)
     absorbed_v[...] = jnp.zeros_like(absorbed_v)
@@ -167,7 +165,7 @@
     def _(peer):
         @pl.when(peer < PIECES)
         def _():
-            over_seq(QUERY_SUM, rows16(qa_send, peer), rows16(qa_recv, me), peer).start()
+            over_seq(QUERY_SUM, rows(qa_send, peer, 13), rows(qa_recv, me, 13), peer).start()
 
     @pl.when(me < PIECES)
     def _():
@@ -175,7 +173,7 @@
             pl.ds(pl.multiple_of(me * 16, 16), 16), :
         ]
 
-        arrived(QUERY_SUM, qa_recv, 15 * 16)
+        arrived(QUERY_SUM, qa_recv, 15 * 13)
 
         total = qa_recv[0:16, :]
         for i in range(1, SEQ):
@@ -186,9 +184,9 @@
 
         @each_peer
         def _(peer):
-            over_seq(QUERY_ALL, rows16(qa_all, me), rows16(qa_all, me), peer).start()
-
-    either(QUERY_ALL, qa_all, me < PIECES, PIECES * 16, arrived)
+            over_seq(QUERY_ALL, rows(qa_all, me, ROWS), rows(qa_all, me, ROWS), peer).start()
+
+    either(QUERY_ALL, qa_all, me < PIECES, PIECES, ROWS, arrived)
 
     l_ku.wait()
     for k in range(GROUP_HEADS):
@@ -253,7 +251,7 @@
         @pl.when(owns_head(peer))
         def _():
             over_seq(
-                HEAD_SUM, rows16(hb_send, head_of_owner(peer)), rows16(hb_recv, me), peer
+                HEAD_SUM, rows(hb_send, head_of_owner(peer), 14), rows(hb_recv, me, 14), peer
             ).start()
 
     own_key = jnp.concatenate([qa_all[(10 + t) * 16 : (11 + t) * 16, :] for t in range(3)], axis=1)
@@ -272,7 +270,7 @@
         absorbed = jnp.concatenate([absorbed_v[t, mine, :] for t in range(3)], axis=1)
         own_score = jnp.sum(absorbed * own_key, axis=1, keepdims=True) * scaling
 
-        arrived(HEAD_SUM, hb_recv, 15 * 16)
+        arrived(HEAD_SUM, hb_recv, 15 * 14)
 
         tops = hb_recv[pl.ds(12, 16, stride=16), :].T[0:16, :]
         sums = hb_recv[pl.ds(13, 16, stride=16), :].T[0:16, :]
@@ -288,9 +286,9 @@
 
         @each_peer
         def _(peer):
-            over_seq(HEAD_ALL, rows16(hb_all, k), rows16(hb_all, k), peer).start()
-
-    either(HEAD_ALL, hb_all, owns_head(me), GROUP_HEADS * 16, arrived)
+            over_seq(HEAD_ALL, rows(hb_all, k, ROWS), rows(hb_all, k, ROWS), peer).start()
+
+    either(HEAD_ALL, hb_all, owns_head(me), GROUP_HEADS, ROWS, arrived)
 
     def over_heads(src, dst, peer):
         return pltpu.make_async_remote_copy(
@@ -303,8 +301,15 @@
     heads_out = jnp.concatenate(
         [hb_all[k * 16 : (k + 1) * 16, :] for k in range(GROUP_HEADS)], axis=1
     ).astype(bf16)
-    at_send[...] = lax.dot_general(
+    attn = lax.dot_general(
         heads_out, wo_v[...], (((1,), (1,)), ((), ())), preferred_element_type=f32
+    )
+    tile_lane, tile_sub = iota((8, 128), 1), iota((8, 128), 0)
+    last = jnp.concatenate([attn[:, 256:320], attn[:, 256:320]], axis=1)
+    at_send[:, 0:256] = attn[0:8, 0:256]
+    at_send[:, 256:384] = jnp.where(tile_lane < 64, last[0:8], last[8:16])
+    at_send[:, 384:512] = jnp.where(
+        tile_sub < 4, attn[8:16, 0:128], pltpu.roll(attn[8:16, 128:256], 4, 0)
     )
     for j in range(1, heads_size):
         peer = lax.rem(hme + j, heads_size)
@@ -317,7 +322,12 @@
     attn = at_recv[0]
     for h in range(1, heads_size):
         attn = attn + at_recv[h]
-    updated = states_v[...] + attn
+    upper = attn[:, 0:320]
+    low = attn[:, 384:512]
+    lower8 = jnp.concatenate(
+        [low, pltpu.roll(low, 4, 0), pltpu.roll(attn[:, 256:384], 64, 1)[:, 0:64]], axis=1
+    )
+    updated = states_v[...] + jnp.concatenate([upper, lower8], axis=0)
     new_hidden[...] = updated[0:ROWS].astype(bf16)
     sq_send[...] = as_row(jnp.sum(updated * updated, axis=1, keepdims=True))
 
@@ -355,28 +365,85 @@
         def _():
             last_piece()
 
-    @each_peer
-    def _(peer):
-        any_piece(peer)
-        over_seq(VOCAB_SUM, vd_send.at[peer], vd_recv.at[me], peer).start()
+    def at(over_y, over_z):
+        return lax.rem(lax.div(me, 8) + over_y, 2) * 8 + lax.rem(lax.rem(me, 8) + over_z, 8)
+
+    def each_side(step):
+        @pl.loop(0, 6)
+        def _(j):
+            t, back = lax.div(j, 2), lax.rem(j, 2)
+            step((1 - back) * (3 - t) + back * (5 + t))
+
+    direct = core == 0
+    by_half = core == 1
+
+    @pl.when(direct)
+    def _():
+        @each_peer
+        def _(peer):
+            any_piece(peer)
+            over_seq(VOCAB_SUM, vd_send.at[peer], vd_recv.at[me], peer).start()
+
+    @pl.when(by_half)
+    def _():
+        @each_side
+        def _(over_z):
+            any_piece(at(1, over_z))
+            pltpu.make_async_remote_copy(
+                src_ref=vd_send.at[at(1, over_z)], dst_ref=vd_half.at[over_z],
+                send_sem=send_sem.at[VOCAB_HALF], recv_sem=half_sem.at[over_z],
+                device_id={"seq": at(1, 0)}, device_id_type=MESH,
+            ).start()
+
+        @pl.loop(0, 3)
+        def _(j):
+            peer = at(1 - lax.rem(j, 2), 4 - 4 * lax.div(j, 2))
+            any_piece(peer)
+            over_seq(VOCAB_SUM, vd_send.at[peer], vd_recv.at[me], peer).start()
+
+        @each_side
+        def _(over_z):
+            any_piece(at(0, over_z))
 
     any_piece(me)
     vd_recv[me] = vd_send[me]
     sq_recv[me] = sq_send[...]
-
-    @pl.when(core == 0)
+    @pl.when(by_half)
+    def _():
+        @each_side
+        def _(over_z):
+            peer = at(0, over_z)
+            half = vd_half.at[over_z]
+            pltpu.make_async_copy(half, half, half_sem.at[over_z]).wait()
+            vd_send[peer] = vd_send[peer] + vd_half[over_z]
+            over_seq(VOCAB_SUM, vd_send.at[peer], vd_recv.at[me], peer).start()
+
+    @pl.when(direct)
     def _():
         sent(VOCAB_SUM, vd_send, 15)
         pl.semaphore_signal(turn_sem, inc=1, device_id={"batch": partner}, device_id_type=MESH)
 
     arrived(SQUARES, sq_recv, 15)
-    arrived(VOCAB_SUM, vd_recv, 15)
+    @pl.when(direct)
+    def _():
+        arrived(VOCAB_SUM, vd_recv, 15)
+        share = vd_recv[0]
+        for i in range(1, SEQ):
+            share = share + vd_recv[i]
+        vd_half[0] = share
+
+    @pl.when(by_half)
+    def _():
+        arrived(VOCAB_SUM, vd_recv, 9)
+        share = vd_recv[me] + vd_recv[at(1, 0)] + vd_recv[at(1, 4)]
+        for over_z in range(1, 8):
+            share = share + vd_recv[at(0, over_z)]
+        vd_half[0] = share
 
     square_total = sq_recv[0]
-    share = vd_recv[0]
     for i in range(1, SEQ):
         square_total = square_total + sq_recv[i]
-        share = share + vd_recv[i]
+    share = vd_half[0]
     inv = lax.rsqrt(square_total / D + epsilon)
     sub = iota((8, 128), 0)
     inv_top = as_column(inv, sub)
@@ -393,10 +460,30 @@
     def _():
         pl.semaphore_wait(turn_sem, 1)
 
-    def send_logits(peer):
+    def send_logits(over_y, over_z):
+        over_seq(VOCAB_ALL, vd_all.at[me], vd_all.at[me], at(over_y, over_z)).start()
+
+    def send_near(over_z):
+        pltpu.make_async_remote_copy(
+            src_ref=vd_all.at[me], dst_ref=vd_all.at[me],
+            send_sem=send_sem.at[VOCAB_ALL], recv_sem=near_sem.at[8 - over_z],
+            device_id={"seq": at(0, over_z)}, device_id_type=MESH,
+        ).start()
+
+    near = [d for t in range(NEAR, 0, -1) for d in (t, 8 - t)]
+    far = [d for t in range(3, NEAR, -1) for d in (t, 8 - t)]
+
+    def send_direct(peer):
         over_seq(VOCAB_ALL, vd_all.at[me], vd_all.at[me], peer).start()
 
-    each_peer(send_logits, 0, 4)
+    @pl.when(direct)
+    def _():
+        each_peer(send_direct, 0, 2)
+
+    @pl.when(by_half)
+    def _():
+        for over_z in near[:2]:
+            send_near(over_z)
 
     l_draft.wait()
     sub1 = iota((8, 1), 0)
@@ -457,31 +544,57 @@
     for j in range(1, heads_size):
         send_stats(me, j)
 
-    each_peer(send_logits, 4, SEQ - 1)
-
-    either(QUERY_SUM, qa_send, me < PIECES, PIECES * 16, sent)
+    @pl.when(direct)
+    def _():
+        each_peer(send_direct, 2, SEQ - 1)
+
+    @pl.when(by_half)
+    def _():
+        send_logits(1, 4)
+        for over_z in far:
+            send_logits(1, over_z)
+        for over_z in near[2:]:
+            send_near(over_z)
+        send_logits(0, 4)
+        for over_z in far:
+            send_logits(0, over_z)
+        send_logits(1, 0)
+        for over_z in near[::-1]:
+            there = vd_all.at[at(0, over_z)]
+            pltpu.make_async_copy(there, there, near_sem.at[over_z]).wait()
+            over_seq(VOCAB_ALL, there, there, at(1, 0)).start()
+
+    either(QUERY_SUM, qa_send, me < PIECES, PIECES, 13, sent)
 
     @pl.when(me < PIECES)
     def _():
-        sent(QUERY_ALL, qa_recv, 15 * 16)
-
-    either(HEAD_SUM, hb_send, owns_head(me), GROUP_HEADS * 16, sent)
+        sent(QUERY_ALL, qa_recv, 15 * ROWS)
+
+    either(HEAD_SUM, hb_send, owns_head(me), GROUP_HEADS, 14, sent)
 
     @pl.when(owns_head(me))
     def _():
-        sent(HEAD_ALL, hb_recv, 15 * 16)
+        sent(HEAD_ALL, hb_recv, 15 * ROWS)
 
     sent(SQUARES, sq_recv, 15)
 
-    @pl.when(core == 1)
-    def _():
-        sent(VOCAB_SUM, vd_send, 15)
+    @pl.when(by_half)
+    def _():
+        sent(VOCAB_SUM, vd_send, 9)
+        sent(VOCAB_HALF, vd_send, 6)
 
     for j in range(1, heads_size):
         peer = lax.rem(hme + j, heads_size)
         pltpu.make_async_copy(at_send, at_send, x_send_sem.at[peer]).wait()
 
-    arrived(VOCAB_ALL, vd_all, 15)
+    @pl.when(direct)
+    def _():
+        arrived(VOCAB_ALL, vd_all, 15)
+
+    @pl.when(by_half)
+    def _():
+        arrived(VOCAB_ALL, vd_all, 15 - 2 * NEAR)
+
     arrived(STATS, st_recv, heads_size * SEQ - 1)
     every = [st_recv[i] for i in range(heads_size * SEQ)]
     highest = functools.reduce(jnp.maximum, every)
@@ -569,20 +682,23 @@
                 pltpu.VMEM((256, 128), f32),
                 pltpu.VMEM((160, 128), f32),
                 pltpu.VMEM((160, 128), f32),
-                pltpu.VMEM((16, RANK), f32),
-                pltpu.VMEM((heads_size, 16, RANK), f32),
+                pltpu.VMEM((8, 512), f32),
+                pltpu.VMEM((heads_size, 8, 512), f32),
                 pltpu.VMEM((1, 128), f32),
                 pltpu.VMEM((SEQ, 1, 128), f32),
                 pltpu.VMEM((SEQ, 8, 768), f32),
                 pltpu.VMEM((SEQ, 8, 768), f32),
+                pltpu.VMEM((8, 8, 768), f32),
                 pltpu.VMEM((1, 128), f32),
                 pltpu.VMEM((heads_size * SEQ, 1, 128), f32),
                 pltpu.SemaphoreType.DMA((12,)),
-                pltpu.SemaphoreType.DMA((8,)),
-                pltpu.SemaphoreType.DMA((8,)),
+                pltpu.SemaphoreType.DMA((9,)),
+                pltpu.SemaphoreType.DMA((9,)),
                 pltpu.SemaphoreType.DMA((heads_size,)),
                 pltpu.SemaphoreType.DMA((heads_size,)),
                 pltpu.SemaphoreType.REGULAR,
+                pltpu.SemaphoreType.DMA((8,)),
+                pltpu.SemaphoreType.DMA((8,)),
             ],
             compiler_params=pltpu.CompilerParams(
                 collective_id=0, has_side_effects=True, vmem_limit_bytes=48 * 1024 * 1024

time: 61.2 us -> 60.7 us (level)
  no operation moved by 1% of the time
where the time goes in v4:
time: 60.7 us; the launch traced here: 60.5 us
  Pallas kernels  59.9 us (99%)
  between operations  0.64 us (1%)
    pallas_call x1, Pallas kernels, body(): pl.pallas_call(functools.partial(kernel, heads_size), name='decode_step',...  59 us

profile of v4, /device:TPU:2, one launch (start us, length us, event | category | flops | bytes accessed | tf_op | source)
XLA Modules:
  0.0 60.5 jit_solution(16316871512463780620)
XLA Ops:
  0.6 59.0 %decode_step.1 = (bf16[12,320]{1,0:T(8,128)(2,1)S(1)}, f32[16,8,768]{2,1,0:T(8,128)S(1)}, f32[8,128]{1,0:T(8,128)S(1)}, f32[1,128]{1,0:T(1,128)S(1)}) custom-call(bf16[12,320]{1,0:T(8,128)(2,1)} %hidden.1, s32[12]{0:T(128)} %lengths.1, s32[12]{0:T(128)} %drafts.1, f32[320]{0:T(512)} %gain.1, bf16[320,1280]{1,0:T(8,128)(2,1)} %wq.1, ...), custom_call_target="tpu_custom_call" | custom-call | tf_op jit(solution)/shard_map/decode_step/pallas_call | solution.py:651
  59.6 0.9 %outputs.1 = (bf16[12,320]{1,0:T(8,128)(2,1)}, f32[12,8000]{1,0:T(8,128)}, f32[12]{0:T(128)}) custom-call(bf16[12,320]{1,0:T(8,128)(2,1)S(1)} %get-tuple-element.7.new_hidden, f32[16,8,768]{2,1,0:T(8,128)S(1)} %get-tuple-element.8.logits, f32[8,128]{1,0:T(8,128)S(1)} %get-tuple-element.9.logs, f32[1,128]{1,0:T(1,128)S(1)} %get-tuple-element.10.draft), custom_call_target="tpu_custom_call" | custom-call | tf_op jit(solution)/shard_map/outputs/pallas_call | solution.py:711

commit v5 on v4

--- a/solution.py
+++ b/solution.py
@@ -18,7 +18,7 @@
 WIDE = 512
 VOCAB_LOCAL = 8000
 PIECES = 15
-NEAR = 3
+NEAR = 2
 TAIL = VOCAB_LOCAL - 15 * WIDE
 
 MESH = pl.DeviceIdType.MESH
@@ -536,8 +536,8 @@
             device_id={"seq": peer, "heads": lax.rem(hme + j, heads_size)}, device_id_type=MESH,
         ).start()
 
-    @each_peer
-    def _(peer):
+    for i in range(SEQ - 1):
+        peer = peer_at(i)
         for j in range(heads_size):
             send_stats(peer, j)
 

time: 60.7 us -> 60.7 us (level)
  no operation moved by 1% of the time
where the time goes in v5:
time: 60.7 us; the launch traced here: 60.4 us
  Pallas kernels  59.8 us (99%)
  between operations  0.64 us (1%)
    pallas_call x1, Pallas kernels, body(): pl.pallas_call(functools.partial(kernel, heads_size), name='decode_step',...  58.9 us

profile of v5, /device:TPU:2, one launch (start us, length us, event | category | flops | bytes accessed | tf_op | source)
XLA Modules:
  0.0 60.4 jit_solution(10644437464622052368)
XLA Ops:
  0.6 58.9 %decode_step.1 = (bf16[12,320]{1,0:T(8,128)(2,1)S(1)}, f32[16,8,768]{2,1,0:T(8,128)S(1)}, f32[8,128]{1,0:T(8,128)S(1)}, f32[1,128]{1,0:T(1,128)S(1)}) custom-call(bf16[12,320]{1,0:T(8,128)(2,1)} %hidden.1, s32[12]{0:T(128)} %lengths.1, s32[12]{0:T(128)} %drafts.1, f32[320]{0:T(512)} %gain.1, bf16[320,1280]{1,0:T(8,128)(2,1)} %wq.1, ...), custom_call_target="tpu_custom_call" | custom-call | tf_op jit(solution)/shard_map/decode_step/pallas_call | solution.py:651
  59.5 0.9 %outputs.1 = (bf16[12,320]{1,0:T(8,128)(2,1)}, f32[12,8000]{1,0:T(8,128)}, f32[12]{0:T(128)}) custom-call(bf16[12,320]{1,0:T(8,128)(2,1)S(1)} %get-tuple-element.7.new_hidden, f32[16,8,768]{2,1,0:T(8,128)S(1)} %get-tuple-element.8.logits, f32[8,128]{1,0:T(8,128)S(1)} %get-tuple-element.9.logs, f32[1,128]{1,0:T(1,128)S(1)} %get-tuple-element.10.draft), custom_call_target="tpu_custom_call" | custom-call | tf_op jit(solution)/shard_map/outputs/pallas_call | solution.py:711
